TPU v7x, 8 devices: a whole 2x2x1 slice. The times are simulated.
8 devices in a mesh: dp: 2 (over z, y), sh: 4 (over x, core).
Axes of the slice: x: 2, y: 2, z: 1, core: 2. Of those that a mesh axis runs over, the one named last changes fastest.
Arguments:
- k_prefill: bfloat16 [24, 10240, 4, 256], P('dp', None, 'sh'), parts along dimension 0
- v_prefill: bfloat16 [24, 10240, 4, 256], P('dp', None, 'sh'), parts along dimension 0
- lengths: int32 [24], P('dp'), parts along dimension 0
- residual: bfloat16 [24, 2304], P(('dp', 'sh')), parts along dimension 0
- norm_gain: bfloat16 [2304], replicated
- w_query: bfloat16 [2304, 2048], replicated
- w_key: bfloat16 [2304, 1024], replicated
- w_value: bfloat16 [2304, 1024], replicated
- w_out: bfloat16 [2048, 2304], replicated
Outputs:
- output 1: bfloat16 [24, 2304], P(('dp', 'sh')), parts along dimension 0
- output 2: bfloat16 [24, 4096, 4, 256], P(('dp', 'sh')), parts along dimension 0
- output 3: bfloat16 [24, 4096, 4, 256], P(('dp', 'sh')), parts along dimension 0
There are 2 independent parts. A program takes and returns all parts, laid end to end along the dimension named above; an argument that names none is the same for every part.
All inputs are finite; a program needn't handle non-finite values.
Results may differ from a plain program's by a relative error of at most 0.0047.
Values are sent between devices in bfloat16 or wider.
A program may use at most 1 GiB of HBM per device.

v0:
```python
import jax
import jax.numpy as jnp
from jax import lax
from jax.sharding import PartitionSpec as P

WINDOW = 4096
THETA = 10000.0
EPS = 1e-5


def rolling_rows(prefill, lengths):
    def one_row(row_vals, row_len):
        first_pos = jnp.maximum(row_len - WINDOW, 0)
        win_vals = lax.dynamic_slice_in_dim(row_vals, first_pos, WINDOW, axis=0)
        positions = first_pos + jnp.arange(WINDOW, dtype=jnp.int32)
        win_vals = jnp.where((positions < row_len)[:, None, None], win_vals, jnp.zeros((), win_vals.dtype))
        doubled = jnp.concatenate([win_vals, win_vals], axis=0)
        return lax.dynamic_slice_in_dim(doubled, WINDOW - first_pos % WINDOW, WINDOW, axis=0)
    return jax.vmap(one_row)(prefill, lengths)


def rotate(heads, positions):
    head_dim = heads.shape[-1]
    half_dim = head_dim // 2
    inv_freq = THETA ** (-2.0 * jnp.arange(half_dim, dtype=jnp.float32) / head_dim)
    angles = positions.astype(jnp.float32).reshape(positions.shape + (1,) * (heads.ndim - 1)) * inv_freq
    cos_part = jnp.cos(angles)
    sin_part = jnp.sin(angles)
    first_half = heads[..., :half_dim].astype(jnp.float32)
    second_half = heads[..., half_dim:].astype(jnp.float32)
    return jnp.concatenate([first_half * cos_part - second_half * sin_part, second_half * cos_part + first_half * sin_part], axis=-1).astype(jnp.bfloat16)


def decode_rows(residual, lengths, k_cache, v_cache, norm_gain, w_query, w_key, w_value, w_out):
    num_rows = residual.shape[0]
    kv_heads = k_cache.shape[2]
    head_dim = k_cache.shape[3]
    q_group = w_query.shape[1] // (kv_heads * head_dim)
    resid_f32 = residual.astype(jnp.float32)
    inv_rms = lax.rsqrt(jnp.mean(resid_f32 * resid_f32, axis=-1, keepdims=True) + EPS)
    normed = (resid_f32 * inv_rms * norm_gain.astype(jnp.float32)).astype(jnp.bfloat16)
    q_heads = jnp.dot(normed, w_query, preferred_element_type=jnp.float32).astype(jnp.bfloat16).reshape(num_rows, kv_heads, q_group, head_dim)
    k_new = jnp.dot(normed, w_key, preferred_element_type=jnp.float32).astype(jnp.bfloat16).reshape(num_rows, kv_heads, head_dim)
    v_new = jnp.dot(normed, w_value, preferred_element_type=jnp.float32).astype(jnp.bfloat16).reshape(num_rows, kv_heads, head_dim)
    q_heads = rotate(q_heads, lengths)
    k_new = rotate(k_new, lengths)
    slot_ids = jnp.arange(WINDOW, dtype=jnp.int32)
    new_slot = (slot_ids[None, :] == (lengths % WINDOW)[:, None])[:, :, None, None]
    k_cache = jnp.where(new_slot, k_new[:, None], k_cache)
    v_cache = jnp.where(new_slot, v_new[:, None], v_cache)
    live_slot = (lengths[:, None] - jnp.remainder(lengths[:, None] - slot_ids[None, :], WINDOW)) >= 0
    scores = jnp.einsum('rkgd,rwkd->rkgw', q_heads, k_cache, preferred_element_type=jnp.float32) / head_dim ** 0.5
    scores = jnp.where(live_slot[:, None, None, :], scores, -jnp.inf)
    exp_scores = jnp.exp(scores - jnp.max(scores, axis=-1, keepdims=True))
    weights = (exp_scores / jnp.sum(exp_scores, axis=-1, keepdims=True)).astype(jnp.bfloat16)
    attn_out = jnp.einsum('rkgw,rwkd->rkgd', weights, v_cache, preferred_element_type=jnp.float32).astype(jnp.bfloat16).reshape(num_rows, kv_heads * q_group * head_dim)
    resid_out = (resid_f32 + jnp.dot(attn_out, w_out, preferred_element_type=jnp.float32)).astype(jnp.bfloat16)
    return resid_out, k_cache, v_cache


def solution(mesh):
    head_spec = P('dp', None, 'sh', None)
    row_spec = P(('dp', 'sh'))
    full_spec = P(None, None)

    def per_device(k_prefill, v_prefill, lengths, residual, norm_gain, w_query, w_key, w_value, w_out):
        num_rows = residual.shape[0]
        my_lengths = lax.dynamic_slice_in_dim(lengths, lax.axis_index('sh') * num_rows, num_rows)
        k_rows = lax.all_to_all(k_prefill, 'sh', 0, 2, tiled=True)
        v_rows = lax.all_to_all(v_prefill, 'sh', 0, 2, tiled=True)
        k_cache = rolling_rows(k_rows, my_lengths)
        v_cache = rolling_rows(v_rows, my_lengths)
        return decode_rows(residual, my_lengths, k_cache, v_cache, norm_gain, w_query, w_key, w_value, w_out)
    return jax.shard_map(per_device, mesh=mesh, in_specs=(head_spec, head_spec, P('dp'), P(('dp', 'sh'), None), P(None), full_spec, full_spec, full_spec, full_spec), out_specs=(P(('dp', 'sh'), None), row_spec, row_spec), check_vma=False)
```

profile of v0, /device:TPU:0, one launch (start us, length us, event | category | flops | bytes accessed | tf_op | source)
XLA Modules:
  0.0 1823.9 jit_solution(886188647815451660)
XLA Ops:
  0.6 708.7 %all_to_all.36 = bf16[12,10240,1,256]{3,1,2,0:T(8,128)(2,1)} all-to-all(bf16[12,10240,1,256]{3,1,2,0:T(8,128)(2,1)} %param.10), channel_id=1, replica_groups=mesh['dp'=2,'sh'=4] {'sh'}, dimensions={0} | all-to-all | bytes 125829120 | tf_op jit(solution)/shard_map/all_to_all | solution.py:70
  709.4 12.9 all-to-all-start
  722.5 0.7 copy.30
  723.3 3.1 convolution_convert_fusion.2
  726.4 3.1 convolution_convert_fusion.1
  730.1 5.0 convolution_convert_fusion
  736.6 0.8 fusion.20
  737.4 8.6 broadcast.224.clone.1
  746.0 69.1 %while.6 = (s32[]{:T(128)}, bf16[3,10240,4,256]{3,1,0,2:T(8,128)(2,1)}, s32[3,4]{1,0:T(4,128)S(1)}, bf16[3,4096,4,256]{3,2,1,0:T(4,128)(2,1)}, s32[]{:T(128)}) while((s32[]{:T(128)}, bf16[3,10240,4,256]{3,1,0,2:T(8,128)(2,1)}, s32[3,4]{1,0:T(4,128)S(1)}, bf16[3,4096,4,256]{3,2,1,0:T(4,128)(2,1)}, s32[]{:T(128)}) %tuple.102), condition=%wide.while_cond.2, body=%wide.while_body.2.sunk | while | flops 2 | bytes 33555064 | solution.py:14
  746.6 10.2 constant_dynamic-slice_fusion.16
  756.9 12.1 copy_dynamic-update-slice_fusion.5
  769.6 10.2 constant_dynamic-slice_fusion.16
  779.9 12.1 copy_dynamic-update-slice_fusion.5
  792.7 10.2 constant_dynamic-slice_fusion.16
  802.9 12.1 copy_dynamic-update-slice_fusion.5
  815.0 584.3 %all-to-all-done = bf16[12,10240,1,256]{3,1,2,0:T(8,128)(2,1)} async-done(((bf16[12,10240,1,256]{3,1,2,0:T(8,128)(2,1)}), bf16[12,10240,1,256]{3,1,2,0:T(8,128)(2,1)}, u32[]{:S(2)}, u32[]{:S(2)}) %all-to-all-start) | async-done | bytes 62914592 | tf_op jit(solution)/shard_map/all_to_all | solution.py:69
  1399.3 8.6 broadcast.224.clone
  1407.9 68.6 %while.4 = (s32[]{:T(128)}, bf16[3,10240,4,256]{3,1,0,2:T(8,128)(2,1)}, s32[3,4]{1,0:T(4,128)S(1)}, bf16[3,4096,4,256]{3,2,1,0:T(4,128)(2,1)}, s32[]{:T(128)}) while((s32[]{:T(128)}, bf16[3,10240,4,256]{3,1,0,2:T(8,128)(2,1)}, s32[3,4]{1,0:T(4,128)S(1)}, bf16[3,4096,4,256]{3,2,1,0:T(4,128)(2,1)}, s32[]{:T(128)}) %tuple.105), condition=%wide.while_cond, body=%wide.while_body.sunk | while | flops 2 | bytes 33555064 | solution.py:14
  1408.0 0.7 fusion.61
  1408.6 10.1 constant_dynamic-slice_fusion.13
  1418.7 12.1 copy_dynamic-update-slice_fusion.4
  1430.8 0.7 fusion.61
  1431.5 10.1 constant_dynamic-slice_fusion.13
  1441.6 12.1 copy_dynamic-update-slice_fusion.4
  1453.7 0.7 fusion.61
  1454.4 10.1 constant_dynamic-slice_fusion.13
  1464.4 12.1 copy_dynamic-update-slice_fusion.4
  1476.6 40.4 %broadcast_select_fusion.1 = (bf16[3,4096,4,256]{3,2,1,0:T(4,128)(2,1)}, bf16[3,4096,4,256]{3,2,1,0:T(4,128)(2,1)}) fusion(bf16[3,4096,4,256]{3,2,1,0:T(4,128)(2,1)} %get-tuple-element.10, pred[3,4096]{1,0:T(4,128)(4,1)S(1)} %get-tuple-element.136, bf16[3,4096,4,256]{3,2,1,0:T(4,128)(2,1)} %get-tuple-element.26), kind=kLoop, calls=%fused_computation.18 | loop fusion | flops 25165824 | bytes 100675584 | tf_op jit(solution)/shard_map/vmap(jit(_where))/select_n | solution.py:16
  1517.0 78.8 %pad_maximum_fusion.1 = bf16[3,8192,4,256]{3,2,1,0:T(4,128)(2,1)} fusion(bf16[3,4096,4,256]{3,2,1,0:T(4,128)(2,1)} %get-tuple-element.130), kind=kLoop, calls=%fused_computation.12 | loop fusion | flops 25165824 | bytes 75497472 | tf_op jit(solution)/shard_map/vmap()/concatenate | solution.py:17
  1595.8 8.6 broadcast.224.clone.3
  1604.4 30.1 %while.7 = (s32[]{:T(128)}, bf16[3,8192,4,256]{3,2,1,0:T(4,128)(2,1)}, s32[3,4]{1,0:T(4,128)S(1)}, bf16[3,4096,4,256]{3,2,1,0:T(4,128)(2,1)}, s32[]{:T(128)}) while((s32[]{:T(128)}, bf16[3,8192,4,256]{3,2,1,0:T(4,128)(2,1)}, s32[3,4]{1,0:T(4,128)S(1)}, bf16[3,4096,4,256]{3,2,1,0:T(4,128)(2,1)}, s32[]{:T(128)}) %tuple.103), condition=%wide.while_cond.3, body=%wide.while_body.3.sunk | while | flops 2 | bytes 16778864 | solution.py:18
  1605.1 9.4 dynamic-slice_dynamic-update-slice_fusion.5
  1614.5 0.7 fusion.64
  1615.1 9.4 dynamic-slice_dynamic-update-slice_fusion.5
  1624.5 0.7 fusion.64
  1625.2 9.4 dynamic-slice_dynamic-update-slice_fusion.5
  1634.6 78.6 %pad_maximum_fusion = bf16[3,8192,4,256]{3,2,1,0:T(4,128)(2,1)} fusion(bf16[3,4096,4,256]{3,2,1,0:T(4,128)(2,1)} %get-tuple-element.129), kind=kLoop, calls=%fused_computation.11 | loop fusion | flops 25165824 | bytes 75497472 | tf_op jit(solution)/shard_map/vmap()/concatenate | solution.py:17
  1713.2 8.6 broadcast.224.clone.2
  1721.8 30.1 %while.5 = (s32[]{:T(128)}, bf16[3,8192,4,256]{3,2,1,0:T(4,128)(2,1)}, s32[3,4]{1,0:T(4,128)S(1)}, bf16[3,4096,4,256]{3,2,1,0:T(4,128)(2,1)}, s32[]{:T(128)}) while((s32[]{:T(128)}, bf16[3,8192,4,256]{3,2,1,0:T(4,128)(2,1)}, s32[3,4]{1,0:T(4,128)S(1)}, bf16[3,4096,4,256]{3,2,1,0:T(4,128)(2,1)}, s32[]{:T(128)}) %tuple.104), condition=%wide.while_cond.1, body=%wide.while_body.1.sunk | while | flops 2 | bytes 16778864 | solution.py:18
  1722.5 9.4 dynamic-slice_dynamic-update-slice_fusion.4
  1731.9 0.7 fusion.62
  1732.6 9.4 dynamic-slice_dynamic-update-slice_fusion.4
  1741.9 0.7 fusion.62
  1742.6 9.4 dynamic-slice_dynamic-update-slice_fusion.4
  1752.0 38.9 %broadcast_select_fusion.3 = (bf16[3,4096,4,256]{3,2,1,0:T(4,128)(2,1)}, bf16[3,4096,4,256]{3,2,1,0:T(4,128)(2,1)}) fusion(bf16[3,4096,4,256]{3,2,1,0:T(4,128)(2,1)} %get-tuple-element.18, pred[3,4096]{1,0:T(4,128)(4,1)S(1)} %copy-done.2, bf16[3,4,256]{2,1,0:T(4,128)(2,1)S(1)} %copy-done.4, bf16[3,4096,4,256]{3,2,1,0:T(4,128)(2,1)} %get-tuple-element.34, ...), kind=kLoop, calls=%fused_computation.20 | loop fusion | flops 25165824 | bytes 100687872 | tf_op jit(solution)/shard_map/jit(_where)/select_n | solution.py:49
  1791.0 15.5 fusion.47
  1806.5 11.7 fusion.14
  1818.2 5.6 fusion.13
  (56 shorter events, 5.7 us)
Async XLA Ops:
  709.4 12.9 copy-start.10
  709.4 13.8 copy-start.8
  709.4 13.8 copy-start
  709.4 690.0 %all-to-all-start = ((bf16[12,10240,1,256]{3,1,2,0:T(8,128)(2,1)}), bf16[12,10240,1,256]{3,1,2,0:T(8,128)(2,1)}, u32[]{:S(2)}, u32[]{:S(2)}) async-start(bf16[12,10240,1,256]{3,1,2,0:T(8,128)(2,1)} %param.9), calls=%async_computation | async-start | bytes 125829120 | tf_op jit(solution)/shard_map/all_to_all | solution.py:69
  1595.8 8.6 copy-start.9
  1721.8 30.2 %copy-start.2 = (pred[3,4096]{1,0:T(4,128)(4,1)S(1)}, pred[3,4096]{1,0:T(4,128)(4,1)}, u32[]{:S(2)}) copy-start(pred[3,4096]{1,0:T(4,128)(4,1)} %get-tuple-element.145) | copy-start | bytes 36868
  1721.8 30.2 %copy-start.3 = (bf16[3,4,256]{2,1,0:T(4,128)(2,1)S(1)}, bf16[3,4,256]{2,1,0:T(4,128)(2,1)}, u32[]{:S(2)}) copy-start(bf16[3,4,256]{2,1,0:T(4,128)(2,1)} %broadcast_in_dim.92) | copy-start | bytes 18436
  1721.8 30.2 %copy-start.4 = (bf16[3,4,256]{2,1,0:T(4,128)(2,1)S(1)}, bf16[3,4,256]{2,1,0:T(4,128)(2,1)}, u32[]{:S(2)}) copy-start(bf16[3,4,256]{2,1,0:T(4,128)(2,1)} %pad_maximum_fusion.2) | copy-start | bytes 18436
  1752.0 38.9 %copy-start.5 = (pred[3,4096]{1,0:T(4,128)(4,1)S(1)}, pred[3,4096]{1,0:T(4,128)(4,1)}, u32[]{:S(2)}) copy-start(pred[3,4096]{1,0:T(4,128)(4,1)} %get-tuple-element.135) | copy-start | bytes 36868
  1752.0 38.9 %copy-start.6 = (bf16[3,4,2,128]{3,2,1,0:T(2,128)(2,1)S(1)}, bf16[3,4,2,128]{3,2,1,0:T(2,128)(2,1)}, u32[]{:S(2)}) copy-start(bf16[3,4,2,128]{3,2,1,0:T(2,128)(2,1)} %get-tuple-element.125) | copy-start | bytes 18436
  1752.0 38.9 %copy-start.7 = (bf16[3,4,2,128]{3,2,1,0:T(2,128)(2,1)S(1)}, bf16[3,4,2,128]{3,2,1,0:T(2,128)(2,1)}, u32[]{:S(2)}) copy-start(bf16[3,4,2,128]{3,2,1,0:T(2,128)(2,1)} %get-tuple-element.126) | copy-start | bytes 18436
  1806.5 11.7 copy-start.1
where the time goes:
time: 1830 us; the launch traced here: 1820 us
  blocking collectives  709 us (39%)
  waiting for transfers between devices  584 us (32%)
  other arithmetic  239 us (13%)
  local copies, waits for them, and re-layouts  234 us (13%)
  matrix products  44.1 us (2%)
    all_to_all x1, blocking collectives, per_device(): v_rows = lax.all_to_all(v_prefill, 'sh', 0, 2, tiled=True)  709 us
    all_to_all x1, waiting for transfers between devices, per_device(): k_rows = lax.all_to_all(k_prefill, 'sh', 0, 2, tiled=True)  584 us
    gather x42, local copies, waits for them, and re-layouts  198 us
    concatenate x2, other arithmetic, one_row(): doubled = jnp.concatenate([win_vals, win_vals], axis=0)  157 us
    select_n x1, other arithmetic, one_row(): jnp.where((positions < row_len)[:, None, None], win_vals, jnp.zeros((), w...  40.4 us
    select_n x1, other arithmetic, decode_rows(): k_cache = jnp.where(new_slot, k_new[:, None], k_cache)  38.9 us
  transfers between devices with their start and end apart: 1, of which 1 were waited for; matrix products, arithmetic and copies ran while one was open for 5% of the time, Pallas kernels for 0%

commit v1 on v0

v1 whole, which is shorter than its diff:
```python
import functools

import jax
import jax.numpy as jnp
from jax import lax
from jax.experimental import pallas as pl
from jax.experimental.pallas import tpu as pltpu
from jax.sharding import PartitionSpec as P

WINDOW = 4096
THETA = 10000.0
EPS = 1e-5
BLK = 16
CHUNK = 512
CB = CHUNK // BLK
NCH = WINDOW // CHUNK


def rotate(heads, positions):
    head_dim = heads.shape[-1]
    half_dim = head_dim // 2
    inv_freq = THETA ** (-2.0 * jnp.arange(half_dim, dtype=jnp.float32) / head_dim)
    angles = positions.astype(jnp.float32).reshape(positions.shape + (1,) * (heads.ndim - 1)) * inv_freq
    cos_part = jnp.cos(angles)
    sin_part = jnp.sin(angles)
    first_half = heads[..., :half_dim].astype(jnp.float32)
    second_half = heads[..., half_dim:].astype(jnp.float32)
    return jnp.concatenate([first_half * cos_part - second_half * sin_part, second_half * cos_part + first_half * sin_part], axis=-1).astype(jnp.bfloat16)


def blank(shape, dtype):
    return pl.pallas_call(
        lambda o_ref: None,
        out_shape=jax.ShapeDtypeStruct(shape, dtype),
        out_specs=pl.BlockSpec(memory_space=pl.ANY),
        name="blank",
    )()


def pick_kernel(ways, n_ref, me_ref, *refs):
    x_refs, y_refs, o_refs = refs[:ways], refs[ways:2 * ways], refs[-ways:]
    c = pl.program_id(0)
    s0 = c * CHUNK
    for d in range(ways):
        n = n_ref[d]
        lap, m = n // WINDOW, lax.rem(n, WINDOW)
        cb = m // CHUNK

        @pl.when((c != cb) & ((c < cb) | (lap >= 1)))
        def _():
            o_refs[d][...] = x_refs[d][0]

        @pl.when((c > cb) & (lap == 0))
        def _():
            o_refs[d][...] = jnp.zeros(o_refs[d].shape, o_refs[d].dtype)

        @pl.when(c == cb)
        def _():
            shape = (CB, BLK, 256)
            slots = s0 + BLK * lax.broadcasted_iota(jnp.int32, shape, 0) + lax.broadcasted_iota(jnp.int32, shape, 1)
            old = jnp.where(lap >= 1, y_refs[d][0].astype(jnp.float32), 0.0)
            o_refs[d][...] = jnp.where(slots < m, x_refs[d][0].astype(jnp.float32), old).astype(jnp.bfloat16)


def pick(prefill, lens, rows, after):
    ways = rows.shape[0]
    seq_blocks = prefill.shape[1]

    def x_map(d):
        def index(c, n_ref, r_ref):
            n = n_ref[d]
            lap, m = n // WINDOW, lax.rem(n, WINDOW)
            from_lap = jnp.where(c <= m // CHUNK, lap, jnp.maximum(lap - 1, 0))
            return r_ref[d], jnp.minimum(from_lap * NCH + c, seq_blocks // CB - 1), 0, 0
        return pl.BlockSpec((1, CB, BLK, 256), index)

    def y_map(d):
        def index(c, n_ref, r_ref):
            n = n_ref[d]
            lap, m = n // WINDOW, lax.rem(n, WINDOW)
            return r_ref[d], jnp.maximum(lap - 1, 0) * NCH + m // CHUNK, 0, 0
        return pl.BlockSpec((1, CB, BLK, 256), index)

    return pl.pallas_call(
        functools.partial(pick_kernel, ways),
        grid_spec=pltpu.PrefetchScalarGridSpec(
            num_scalar_prefetch=2,
            grid=(NCH,),
            in_specs=[x_map(d) for d in range(ways)] + [y_map(d) for d in range(ways)] + [pl.BlockSpec(memory_space=pl.ANY)] * len(after),
            out_specs=[pl.BlockSpec((CB, BLK, 256), lambda c, n_ref, r_ref: (c, 0, 0))] * ways,
        ),
        out_shape=[jax.ShapeDtypeStruct((WINDOW // BLK, BLK, 256), prefill.dtype)] * ways,
        compiler_params=pltpu.CompilerParams(dimension_semantics=("arbitrary",), vmem_limit_bytes=60 * 1024 * 1024),
        cost_estimate=pl.CostEstimate(flops=1_000_000, bytes_accessed=16_000_000, transcendentals=0),
        name="pick",
    )(lens, rows, *([prefill] * (2 * ways)), *after)


def assemble_kernel(is_key, ways, n_ref, me_ref, *refs):
    x_refs = refs[:ways]
    new_ref, qp_ref, _, cache_ref, res_ref, acc = refs[ways:]
    c = pl.program_id(0)
    s0 = c * CHUNK
    me = me_ref[0]
    n = n_ref[0]
    lap, m = n // WINDOW, lax.rem(n, WINDOW)

    @pl.when((s0 <= m) & (m < s0 + CHUNK))
    def _():
        b = (m - s0) // BLK
        here = lax.broadcasted_iota(jnp.int32, (BLK, 256), 0) == lax.rem(m, BLK)
        for d in range(ways):
            new = jnp.broadcast_to(new_ref[me ^ d], (BLK, 256))
            x_refs[d][b] = jnp.where(here, new, x_refs[d][b].astype(jnp.float32)).astype(jnp.bfloat16)

    xs = [x_refs[d][...].reshape(CHUNK, 256) for d in range(ways)]
    if is_key:
        cols = s0 + lax.broadcasted_iota(jnp.int32, (8, CHUNK), 1)
        live = (lap >= 1) | (cols <= n)
        for d in range(ways):
            s = lax.dot_general(qp_ref[me ^ d], xs[d], (((1,), (1,)), ((), ())), preferred_element_type=jnp.float32)
            res_ref[me ^ d] = jnp.where(live, s / 16.0, -jnp.inf)
    else:
        @pl.when(c == 0)
        def _():
            acc[...] = jnp.zeros_like(acc)

        for d in range(ways):
            acc[me ^ d] += jnp.dot(qp_ref[me ^ d], xs[d], preferred_element_type=jnp.float32)

        @pl.when(c == NCH - 1)
        def _():
            res_ref[...] = acc[...]

    for bit in (1, 2):
        swap = (me & bit) != 0
        xs = [jnp.where(swap, xs[h ^ bit], xs[h]) for h in range(ways)]
    cache_ref[0] = jnp.stack(xs, axis=1)


def assemble(is_key, row, n, me, parts, new, qp, cache):
    ways = len(parts)
    whole = lambda *shape: pl.BlockSpec(shape, lambda c, n_ref, me_ref: (0,) * len(shape))
    by_chunk = pl.BlockSpec((ways, 8, CHUNK), lambda c, n_ref, me_ref: (0, 0, c))
    if is_key:
        qp_spec = whole(ways, 8, 256)
        res_shape, res_spec = jax.ShapeDtypeStruct((ways, 8, WINDOW), jnp.float32), by_chunk
    else:
        qp_spec = by_chunk
        res_shape, res_spec = jax.ShapeDtypeStruct((ways, 8, 256), jnp.float32), whole(ways, 8, 256)
    return pl.pallas_call(
        functools.partial(assemble_kernel, is_key, ways),
        grid_spec=pltpu.PrefetchScalarGridSpec(
            num_scalar_prefetch=2,
            grid=(NCH,),
            in_specs=[pl.BlockSpec((CB, BLK, 256), lambda c, n_ref, me_ref: (c, 0, 0))] * ways + [whole(ways, 1, 256), qp_spec, pl.BlockSpec(memory_space=pl.ANY)],
            out_specs=[pl.BlockSpec((1, CHUNK, ways, 256), lambda c, n_ref, me_ref: (row, c, 0, 0)), res_spec],
            scratch_shapes=[pltpu.VMEM((ways, 8, 256), jnp.float32)],
        ),
        out_shape=[jax.ShapeDtypeStruct(cache.shape, cache.dtype), res_shape],
        input_output_aliases={2 + ways + 2: 0},
        compiler_params=pltpu.CompilerParams(dimension_semantics=("arbitrary",), vmem_limit_bytes=60 * 1024 * 1024),
        cost_estimate=pl.CostEstimate(flops=20_000_000_000, bytes_accessed=16_000_000, transcendentals=0),
        name="assemble_keys" if is_key else "assemble_values",
    )(n, me, *parts, new, qp, cache)


def solution(mesh):
    head_spec = P('dp', None, 'sh', None)
    row_spec = P(('dp', 'sh'))
    full_spec = P(None, None)
    ways = mesh.shape['sh']

    def per_device(k_prefill, v_prefill, lengths, residual, norm_gain, w_query, w_key, w_value, w_out):
        num_rows = residual.shape[0]
        all_rows, seq = k_prefill.shape[0], k_prefill.shape[1]
        heads = ways
        me = lax.axis_index('sh').astype(jnp.int32)
        my_lengths = lax.dynamic_slice_in_dim(lengths, me * num_rows, num_rows)
        peers = me ^ jnp.arange(ways, dtype=jnp.int32)
        k_blocks = k_prefill.reshape(all_rows, seq // BLK, BLK, 256)
        v_blocks = v_prefill.reshape(all_rows, seq // BLK, BLK, 256)

        stages = []
        for is_key in (True, False):
            for r in range(num_rows):
                rows = peers * num_rows + r
                after = list(stages[-2][1:]) if len(stages) >= 2 else []
                sent = pick(k_blocks if is_key else v_blocks, lengths[rows], rows, after)
                got = [sent[0]] + [lax.ppermute(sent[d], 'sh', [(i, i ^ d) for i in range(ways)]) for d in range(1, ways)]
                stages.append(got)

        resid_f32 = residual.astype(jnp.float32)
        inv_rms = lax.rsqrt(jnp.mean(resid_f32 * resid_f32, axis=-1, keepdims=True) + EPS)
        normed = (resid_f32 * inv_rms * norm_gain.astype(jnp.float32)).astype(jnp.bfloat16)
        q_group = w_query.shape[1] // (heads * 256)
        q_heads = jnp.dot(normed, w_query, preferred_element_type=jnp.float32).astype(jnp.bfloat16).reshape(num_rows, heads, q_group, 256)
        k_new = jnp.dot(normed, w_key, preferred_element_type=jnp.float32).astype(jnp.bfloat16).reshape(num_rows, heads, 256)
        v_new = jnp.dot(normed, w_value, preferred_element_type=jnp.float32).astype(jnp.bfloat16).reshape(num_rows, heads, 256)
        q_heads = rotate(q_heads, my_lengths)
        k_new = rotate(k_new, my_lengths)
        k_new, v_new = k_new.astype(jnp.float32)[:, :, None], v_new.astype(jnp.float32)[:, :, None]
        q_pad = jnp.pad(q_heads, ((0, 0), (0, 0), (0, 8 - q_group), (0, 0)))

        me1 = me.reshape(1)
        cache_shape = (num_rows, WINDOW, heads, 256)
        k_cache, v_cache = blank(cache_shape, jnp.bfloat16), blank(cache_shape, jnp.bfloat16)
        weights, attn = [], []
        for r in range(num_rows):
            k_cache, scores = assemble(True, r, my_lengths[r:r + 1], me1, stages[r], k_new[r], q_pad[r], k_cache)
            exp_scores = jnp.exp(scores - jnp.max(scores, axis=-1, keepdims=True))
            weights.append((exp_scores / jnp.sum(exp_scores, axis=-1, keepdims=True)).astype(jnp.bfloat16))
        for r in range(num_rows):
            v_cache, mixed = assemble(False, r, my_lengths[r:r + 1], me1, stages[num_rows + r], v_new[r], weights[r], v_cache)
            attn.append(mixed[:, :q_group].astype(jnp.bfloat16).reshape(1, heads * q_group * 256))
        attn_out = jnp.concatenate(attn, axis=0)
        resid_out = (resid_f32 + jnp.dot(attn_out, w_out, preferred_element_type=jnp.float32)).astype(jnp.bfloat16)
        return resid_out, k_cache, v_cache
    return jax.shard_map(per_device, mesh=mesh, in_specs=(head_spec, head_spec, P('dp'), P(('dp', 'sh'), None), P(None), full_spec, full_spec, full_spec, full_spec), out_specs=(P(('dp', 'sh'), None), row_spec, row_spec), check_vma=False)
```

time: 1830 us -> 623 us (0.34)
  blocking collectives: 709 us -> 0 us
  other arithmetic: 239 us -> 9.57 us
  local copies, waits for them, and re-layouts: 234 us -> 8.56 us
  waiting for transfers between devices: 584 us -> 395 us
  Pallas kernels: 0 us -> 176 us
  matrix products: 44.1 us -> 16.9 us
    all_to_all x1 -> x0, blocking collectives: 709 us -> none  [per_device(): v_rows = lax.all_to_all(v_prefill, 'sh', 0, 2, tiled=True)]
    all_to_all x1 -> x0, waiting for transfers between devices: 584 us -> none  [per_device(): k_rows = lax.all_to_all(k_prefill, 'sh', 0, 2, tiled=True)]
    ppermute x0 -> x18, waiting for transfers between devices: none -> 395 us  [per_device(): lax.ppermute(sent[d], 'sh', [(i, i ^ d) for i in range(ways)])]
    gather x42 -> x3, local copies, waits for them, and re-layouts: 198 us -> 4.19 us  [per_device(): sent = pick(k_blocks if is_key else v_blocks, lengths[rows], rows, after)]
    pallas_call x0 -> x14, Pallas kernels: none -> 176 us  [the longest x6 114 us: assemble(): pl.pallas_call(functools.partial(assemble_kernel, is_key, ways), grid_spe...]
    concatenate x2 -> x0, other arithmetic: 157 us -> none  [one_row(): doubled = jnp.concatenate([win_vals, win_vals], axis=0)]
    select_n x3 -> x2, other arithmetic: 79.3 us -> 0.02 us  [per_device(): sent = pick(k_blocks if is_key else v_blocks, lengths[rows], rows, after)]
    unnamed x29 -> x14, local copies, waits for them, and re-layouts: 35.3 us -> 0.15 us
  transfers between devices with their start and end apart: 1 -> 18, of which waited for: 1 -> 7; matrix products, arithmetic and copies ran while one was open for 5% -> 4% of each run, Pallas kernels for 0% -> 24%
where the time goes in v1:
time: 623 us; the launch traced here: 621 us
  waiting for transfers between devices  395 us (63%)
  Pallas kernels  176 us (28%)
  matrix products  16.9 us (3%)
  starting transfers between devices  14.2 us (2%)
  other arithmetic  9.57 us (2%)
  local copies, waits for them, and re-layouts  8.56 us (1%)
    ppermute x18, waiting for transfers between devices, per_device(): lax.ppermute(sent[d], 'sh', [(i, i ^ d) for i in range(ways)])  395 us
    pallas_call x6, Pallas kernels, assemble(): pl.pallas_call(functools.partial(assemble_kernel, is_key, ways), grid_spe...  114 us
    pallas_call x6, Pallas kernels, pick(): pl.pallas_call(functools.partial(pick_kernel, ways), grid_spec=pltpu.Pref...  62.2 us
    ppermute x18, starting transfers between devices, per_device(): lax.ppermute(sent[d], 'sh', [(i, i ^ d) for i in range(ways)])  14.2 us
  transfers between devices with their start and end apart: 18, of which 7 were waited for; matrix products, arithmetic and copies ran while one was open for 4% of the time, Pallas kernels for 24%

profile of v1, /device:TPU:0, one launch (start us, length us, event | category | flops | bytes accessed | tf_op | source)
XLA Modules:
  0.0 620.8 jit_solution(13304333496835294129)
XLA Ops:
  0.6 0.5 broadcast_add_fusion.1.me_ref
  1.2 1.8 gather_fusion.1
  3.0 10.6 %pick.6 = (bf16[256,16,256]{2,1,0:T(8,128)(2,1)}, bf16[256,16,256]{2,1,0:T(8,128)(2,1)}, bf16[256,16,256]{2,1,0:T(8,128)(2,1)}, bf16[256,16,256]{2,1,0:T(8,128)(2,1)}) custom-call(s32[4]{0:T(128)} %gather_fusion.1, s32[4]{0:T(128)} %broadcast_add_fusion.1.me_ref, bf16[12,640,16,256]{3,2,1,0:T(8,128)(2,1)} %bitcast.32, bf16[12,640,16,256]{3,2,1,0:T(8,128)(2,1)} %bitcast.33, ...), custom_call_target="tpu_custom_call" | custom-call | flops 1000000 | bytes 16000000 | tf_op jit(solution)/shard_map/pick/pallas_call | solution.py:84
  13.6 0.9 collective-permute-start
  14.5 1.2 gather_fusion
  15.7 0.5 xor_multiply_fusion.me_ref
  16.2 10.0 %pick.8 = (bf16[256,16,256]{2,1,0:T(8,128)(2,1)}, bf16[256,16,256]{2,1,0:T(8,128)(2,1)}, bf16[256,16,256]{2,1,0:T(8,128)(2,1)}, bf16[256,16,256]{2,1,0:T(8,128)(2,1)}) custom-call(s32[4]{0:T(128)} %gather_fusion, s32[4]{0:T(128)} %xor_multiply_fusion.me_ref, bf16[12,640,16,256]{3,2,1,0:T(8,128)(2,1)} %bitcast.43, bf16[12,640,16,256]{3,2,1,0:T(8,128)(2,1)} %bitcast.41, ...), custom_call_target="tpu_custom_call" | custom-call | flops 1000000 | bytes 16000000 | tf_op jit(solution)/shard_map/pick/pallas_call | solution.py:84
  26.3 3.0 collective-permute-start.7
  29.3 1.4 collective-permute-start.1
  30.8 0.7 fusion.50
  31.5 5.0 convolution_convert_fusion
  37.0 0.8 broadcast_add_fusion.me_ref
  38.0 1.2 gather_fusion.2
  39.3 3.1 convolution_convert_fusion.1
  42.4 0.6 convert_bitcast_fusion.1
  43.0 3.1 fusion.19
  46.1 0.6 fusion.49
  46.7 0.6 slice_bitcast_fusion.2
  47.3 118.3 %collective-permute-done.1.refs_9_.refs_2_ = bf16[256,16,256]{2,1,0:T(8,128)(2,1)} collective-permute-done((bf16[256,16,256]{2,1,0:T(8,128)(2,1)}, bf16[256,16,256]{2,1,0:T(8,128)(2,1)}, u32[]{:S(2)}, u32[]{:S(2)}) %collective-permute-start.1) | collective-permute-done | bytes 2097184 | tf_op jit(solution)/shard_map/ppermute | solution.py:190
  165.6 43.6 %collective-permute-done.2.refs_10_.refs_3_ = bf16[256,16,256]{2,1,0:T(8,128)(2,1)} collective-permute-done((bf16[256,16,256]{2,1,0:T(8,128)(2,1)}, bf16[256,16,256]{2,1,0:T(8,128)(2,1)}, u32[]{:S(2)}, u32[]{:S(2)}) %collective-permute-start.2) | collective-permute-done | bytes 2097184 | tf_op jit(solution)/shard_map/ppermute | solution.py:190
  209.2 9.9 %pick.7 = (bf16[256,16,256]{2,1,0:T(8,128)(2,1)}, bf16[256,16,256]{2,1,0:T(8,128)(2,1)}, bf16[256,16,256]{2,1,0:T(8,128)(2,1)}, bf16[256,16,256]{2,1,0:T(8,128)(2,1)}) custom-call(s32[4]{0:T(128)} %gather_fusion, s32[4]{0:T(128)} %xor_multiply_fusion.me_ref, bf16[12,640,16,256]{3,2,1,0:T(8,128)(2,1)} %bitcast.56, bf16[12,640,16,256]{3,2,1,0:T(8,128)(2,1)} %bitcast.57, ...), custom_call_target="tpu_custom_call" | custom-call | flops 1000000 | bytes 16000000 | tf_op jit(solution)/shard_map/pick/pallas_call | solution.py:84
  219.1 0.5 collective-permute-start.3
  219.6 1.8 collective-permute-start.4
  221.4 10.5 %pick.9 = (bf16[256,16,256]{2,1,0:T(8,128)(2,1)}, bf16[256,16,256]{2,1,0:T(8,128)(2,1)}, bf16[256,16,256]{2,1,0:T(8,128)(2,1)}, bf16[256,16,256]{2,1,0:T(8,128)(2,1)}) custom-call(s32[4]{0:T(128)} %gather_fusion.2, s32[4]{0:T(128)} %broadcast_add_fusion.me_ref, bf16[12,640,16,256]{3,2,1,0:T(8,128)(2,1)} %bitcast.48, bf16[12,640,16,256]{3,2,1,0:T(8,128)(2,1)} %bitcast.49, ...), custom_call_target="tpu_custom_call" | custom-call | flops 1000000 | bytes 16000000 | tf_op jit(solution)/shard_map/pick/pallas_call | solution.py:84
  231.9 1.4 collective-permute-start.10
  233.6 18.7 %assemble_keys.3 = (bf16[3,4096,4,256]{3,2,1,0:T(4,128)(2,1)}, f32[4,8,4096]{2,1,0:T(8,128)}) custom-call(s32[1]{0:T(128)} %get-tuple-element.92.n_ref, s32[1]{0:T(128)} %bitcast.me_ref, bf16[256,16,256]{2,1,0:T(8,128)(2,1)} %get-tuple-element.46.refs_0_, ...), custom_call_target="tpu_custom_call", output_to_operand_aliasing={{0}: (8, {})} | custom-call | flops 20000000000 | bytes 16000000 | tf_op jit(solution)/shard_map/assemble_keys/pallas_call | solution.py:151
  252.3 2.3 fusion.17.refs_5_
  254.6 103.4 %collective-permute-done.10.refs_9_.refs_2_ = bf16[256,16,256]{2,1,0:T(8,128)(2,1)S(1)} collective-permute-done((bf16[256,16,256]{2,1,0:T(8,128)(2,1)}, bf16[256,16,256]{2,1,0:T(8,128)(2,1)S(1)}, u32[]{:S(2)}, u32[]{:S(2)}) %collective-permute-start.10) | collective-permute-done | bytes 2097184 | tf_op jit(solution)/shard_map/ppermute | solution.py:190
  358.0 18.7 %assemble_keys.4 = (bf16[3,4096,4,256]{3,2,1,0:T(4,128)(2,1)}, f32[4,8,4096]{2,1,0:T(8,128)}) custom-call(s32[1]{0:T(128)} %get-tuple-element.93.n_ref, s32[1]{0:T(128)} %bitcast.me_ref, bf16[256,16,256]{2,1,0:T(8,128)(2,1)} %get-tuple-element.59.refs_0_, bf16[256,16,256]{2,1,0:T(8,128)(2,1)} %copy-done.1, ...), custom_call_target="tpu_custom_call", output_to_operand_aliasing={{0}: (8, {})} | custom-call | flops 20000000000 | bytes 16000000 | tf_op jit(solution)/shard_map/assemble_keys/pallas_call | solution.py:151
  376.8 2.2 fusion.16.refs_5_
  378.9 22.3 %collective-permute-done.11.refs_10_.refs_3_ = bf16[256,16,256]{2,1,0:T(8,128)(2,1)} collective-permute-done((bf16[256,16,256]{2,1,0:T(8,128)(2,1)}, bf16[256,16,256]{2,1,0:T(8,128)(2,1)}, u32[]{:S(2)}, u32[]{:S(2)}) %collective-permute-start.11) | collective-permute-done | bytes 2097184 | tf_op jit(solution)/shard_map/ppermute | solution.py:190
  401.3 10.7 %pick.10 = (bf16[256,16,256]{2,1,0:T(8,128)(2,1)}, bf16[256,16,256]{2,1,0:T(8,128)(2,1)}, bf16[256,16,256]{2,1,0:T(8,128)(2,1)}, bf16[256,16,256]{2,1,0:T(8,128)(2,1)}) custom-call(s32[4]{0:T(128)} %gather_fusion.1, s32[4]{0:T(128)} %broadcast_add_fusion.1.me_ref, bf16[12,640,16,256]{3,2,1,0:T(8,128)(2,1)} %bitcast.67, bf16[12,640,16,256]{3,2,1,0:T(8,128)(2,1)} %bitcast.65, ...), custom_call_target="tpu_custom_call" | custom-call | flops 1000000 | bytes 16000000 | tf_op jit(solution)/shard_map/pick/pallas_call | solution.py:84
  412.0 0.6 collective-permute-start.12
  412.6 1.8 collective-permute-start.13
  414.5 10.5 %pick.11 = (bf16[256,16,256]{2,1,0:T(8,128)(2,1)}, bf16[256,16,256]{2,1,0:T(8,128)(2,1)}, bf16[256,16,256]{2,1,0:T(8,128)(2,1)}, bf16[256,16,256]{2,1,0:T(8,128)(2,1)}) custom-call(s32[4]{0:T(128)} %gather_fusion.2, s32[4]{0:T(128)} %broadcast_add_fusion.me_ref, bf16[12,640,16,256]{3,2,1,0:T(8,128)(2,1)} %bitcast.72, bf16[12,640,16,256]{3,2,1,0:T(8,128)(2,1)} %bitcast.73, ...), custom_call_target="tpu_custom_call" | custom-call | flops 1000000 | bytes 16000000 | tf_op jit(solution)/shard_map/pick/pallas_call | solution.py:84
  425.2 1.8 collective-permute-start.16
  427.0 19.3 %assemble_values.3 = (bf16[3,4096,4,256]{3,2,1,0:T(4,128)(2,1)}, f32[4,8,256]{2,1,0:T(8,128)}) custom-call(s32[1]{0:T(128)} %get-tuple-element.92.n_ref, s32[1]{0:T(128)} %bitcast.me_ref, bf16[256,16,256]{2,1,0:T(8,128)(2,1)} %get-tuple-element.42.refs_0_, ...), custom_call_target="tpu_custom_call", output_to_operand_aliasing={{0}: (8, {})} | custom-call | flops 20000000000 | bytes 16000000 | tf_op jit(solution)/shard_map/assemble_values/pallas_call | solution.py:151
  446.3 0.8 slice.126
  447.1 18.6 %assemble_keys.5 = (bf16[3,4096,4,256]{3,2,1,0:T(4,128)(2,1)}, f32[4,8,4096]{2,1,0:T(8,128)}) custom-call(s32[1]{0:T(128)} %get-tuple-element.94.n_ref, s32[1]{0:T(128)} %bitcast.me_ref, bf16[256,16,256]{2,1,0:T(8,128)(2,1)} %get-tuple-element.68.refs_0_, ...), custom_call_target="tpu_custom_call", output_to_operand_aliasing={{0}: (8, {})} | custom-call | flops 20000000000 | bytes 16000000 | tf_op jit(solution)/shard_map/assemble_keys/pallas_call | solution.py:151
  465.8 2.2 fusion.15.refs_5_
  468.0 37.4 %collective-permute-done.14.refs_3_ = bf16[256,16,256]{2,1,0:T(8,128)(2,1)} collective-permute-done((bf16[256,16,256]{2,1,0:T(8,128)(2,1)}, bf16[256,16,256]{2,1,0:T(8,128)(2,1)}, u32[]{:S(2)}, u32[]{:S(2)}) %collective-permute-start.14) | collective-permute-done | bytes 2097184 | tf_op jit(solution)/shard_map/ppermute | solution.py:190
  505.4 19.3 %assemble_values.4 = (bf16[3,4096,4,256]{3,2,1,0:T(4,128)(2,1)}, f32[4,8,256]{2,1,0:T(8,128)}) custom-call(s32[1]{0:T(128)} %get-tuple-element.93.n_ref, s32[1]{0:T(128)} %bitcast.me_ref, bf16[256,16,256]{2,1,0:T(8,128)(2,1)} %get-tuple-element.55.refs_0_, bf16[256,16,256]{2,1,0:T(8,128)(2,1)} %collective-permute-done.12.refs_1_, ...), custom_call_target="tpu_custom_call", output_to_operand_aliasing={{0}: (8, {})} | custom-call | flops 20000000000 | bytes 16000000 | tf_op jit(solution)/shard_map/assemble_values/pallas_call | solution.py:151
  524.7 26.3 %collective-permute-done.16.refs_2_ = bf16[256,16,256]{2,1,0:T(8,128)(2,1)} collective-permute-done((bf16[256,16,256]{2,1,0:T(8,128)(2,1)}, bf16[256,16,256]{2,1,0:T(8,128)(2,1)}, u32[]{:S(2)}, u32[]{:S(2)}) %collective-permute-start.16) | collective-permute-done | bytes 2097184 | tf_op jit(solution)/shard_map/ppermute | solution.py:190
  551.0 43.3 %collective-permute-done.17.refs_3_ = bf16[256,16,256]{2,1,0:T(8,128)(2,1)} collective-permute-done((bf16[256,16,256]{2,1,0:T(8,128)(2,1)}, bf16[256,16,256]{2,1,0:T(8,128)(2,1)}, u32[]{:S(2)}, u32[]{:S(2)}) %collective-permute-start.17) | collective-permute-done | bytes 2097184 | tf_op jit(solution)/shard_map/ppermute | solution.py:190
  594.3 19.3 %assemble_values.5 = (bf16[3,4096,4,256]{3,2,1,0:T(4,128)(2,1)}, f32[4,8,256]{2,1,0:T(8,128)}) custom-call(s32[1]{0:T(128)} %get-tuple-element.94.n_ref, s32[1]{0:T(128)} %bitcast.me_ref, bf16[256,16,256]{2,1,0:T(8,128)(2,1)} %get-tuple-element.64.refs_0_, bf16[256,16,256]{2,1,0:T(8,128)(2,1)} %copy-done.6, ...), custom_call_target="tpu_custom_call", output_to_operand_aliasing={{0}: (8, {})} | custom-call | flops 20000000000 | bytes 16000000 | tf_op jit(solution)/shard_map/assemble_values/pallas_call | solution.py:151
  613.6 0.8 slice.124
  614.4 0.8 slice.125
  615.2 5.6 fusion.18
  (54 shorter events, 1.7 us)
Async XLA Ops:
  3.0 11.5 %copy-start = (s32[12]{0:T(128)S(1)}, s32[12]{0:T(128)}, u32[]{:S(2)}) copy-start(s32[12]{0:T(128)} %param.11) | copy-start | bytes 148
  13.6 23.0 %collective-permute-start = (bf16[256,16,256]{2,1,0:T(8,128)(2,1)}, bf16[256,16,256]{2,1,0:T(8,128)(2,1)S(1)}, u32[]{:S(2)}, u32[]{:S(2)}) collective-permute-start(bf16[256,16,256]{2,1,0:T(8,128)(2,1)} %get-tuple-element.39), channel_id=1, source_target_pairs={{0,1},{1,0},{2,3},{3,2},{4,5},{5,4},{6,7},{7,6}} | collective-permute-start | bytes 6291464 | tf_op jit(solution)/shard_map/ppermute | solution.py:190
  16.2 14.4 %copy-start.5 = (bf16[2304]{0:T(1024)(128)(2,1)S(1)}, bf16[2304]{0:T(1024)(128)(2,1)}, u32[]{:S(2)}) copy-start(bf16[2304]{0:T(1024)(128)(2,1)} %param.13) | copy-start | bytes 13828
  16.2 15.2 %copy-start.3 = (bf16[3,2304]{1,0:T(4,128)(2,1)S(1)}, bf16[3,2304]{1,0:T(4,128)(2,1)}, u32[]{:S(2)}) copy-start(bf16[3,2304]{1,0:T(4,128)(2,1)} %param.12) | copy-start | bytes 41476
  26.3 195.1 %collective-permute-start.6 = (bf16[256,16,256]{2,1,0:T(8,128)(2,1)}, bf16[256,16,256]{2,1,0:T(8,128)(2,1)}, u32[]{:S(2)}, u32[]{:S(2)}) collective-permute-start(bf16[256,16,256]{2,1,0:T(8,128)(2,1)} %get-tuple-element.47), channel_id=1, source_target_pairs={{0,1},{1,0},{2,3},{3,2},{4,5},{5,4},{6,7},{7,6}} | collective-permute-start | bytes 6291464 | tf_op jit(solution)/shard_map/ppermute | solution.py:190
  26.3 195.1 %collective-permute-start.7 = (bf16[256,16,256]{2,1,0:T(8,128)(2,1)}, bf16[256,16,256]{2,1,0:T(8,128)(2,1)}, u32[]{:S(2)}, u32[]{:S(2)}) collective-permute-start(bf16[256,16,256]{2,1,0:T(8,128)(2,1)} %get-tuple-element.48), channel_id=1, source_target_pairs={{0,2},{1,3},{2,0},{3,1},{4,6},{5,7},{6,4},{7,5}} | collective-permute-start | bytes 6291464 | tf_op jit(solution)/shard_map/ppermute | solution.py:190
  29.3 192.1 %collective-permute-start.8 = (bf16[256,16,256]{2,1,0:T(8,128)(2,1)}, bf16[256,16,256]{2,1,0:T(8,128)(2,1)}, u32[]{:S(2)}, u32[]{:S(2)}) collective-permute-start(bf16[256,16,256]{2,1,0:T(8,128)(2,1)} %get-tuple-element.49), channel_id=1, source_target_pairs={{0,3},{1,2},{2,1},{3,0},{4,7},{5,6},{6,5},{7,4}} | collective-permute-start | bytes 6291464 | tf_op jit(solution)/shard_map/ppermute | solution.py:190
  29.3 136.4 %collective-permute-start.1 = (bf16[256,16,256]{2,1,0:T(8,128)(2,1)}, bf16[256,16,256]{2,1,0:T(8,128)(2,1)}, u32[]{:S(2)}, u32[]{:S(2)}) collective-permute-start(bf16[256,16,256]{2,1,0:T(8,128)(2,1)} %get-tuple-element.40), channel_id=1, source_target_pairs={{0,2},{1,3},{2,0},{3,1},{4,6},{5,7},{6,4},{7,5}} | collective-permute-start | bytes 6291464 | tf_op jit(solution)/shard_map/ppermute | solution.py:190
  36.6 1.4 copy-start.1
  36.6 172.6 %collective-permute-start.2 = (bf16[256,16,256]{2,1,0:T(8,128)(2,1)}, bf16[256,16,256]{2,1,0:T(8,128)(2,1)}, u32[]{:S(2)}, u32[]{:S(2)}) collective-permute-start(bf16[256,16,256]{2,1,0:T(8,128)(2,1)} %get-tuple-element.41), channel_id=1, source_target_pairs={{0,3},{1,2},{2,1},{3,0},{4,7},{5,6},{6,5},{7,4}} | collective-permute-start | bytes 6291464 | tf_op jit(solution)/shard_map/ppermute | solution.py:190
  219.1 195.3 %collective-permute-start.3 = (bf16[256,16,256]{2,1,0:T(8,128)(2,1)}, bf16[256,16,256]{2,1,0:T(8,128)(2,1)}, u32[]{:S(2)}, u32[]{:S(2)}) collective-permute-start(bf16[256,16,256]{2,1,0:T(8,128)(2,1)} %get-tuple-element.43), channel_id=1, source_target_pairs={{0,1},{1,0},{2,3},{3,2},{4,5},{5,4},{6,7},{7,6}} | collective-permute-start | bytes 6291464 | tf_op jit(solution)/shard_map/ppermute | solution.py:190
  219.6 194.8 %collective-permute-start.4 = (bf16[256,16,256]{2,1,0:T(8,128)(2,1)}, bf16[256,16,256]{2,1,0:T(8,128)(2,1)}, u32[]{:S(2)}, u32[]{:S(2)}) collective-permute-start(bf16[256,16,256]{2,1,0:T(8,128)(2,1)} %get-tuple-element.44), channel_id=1, source_target_pairs={{0,2},{1,3},{2,0},{3,1},{4,6},{5,7},{6,4},{7,5}} | collective-permute-start | bytes 6291464 | tf_op jit(solution)/shard_map/ppermute | solution.py:190
  221.4 193.1 %collective-permute-start.5 = (bf16[256,16,256]{2,1,0:T(8,128)(2,1)}, bf16[256,16,256]{2,1,0:T(8,128)(2,1)}, u32[]{:S(2)}, u32[]{:S(2)}) collective-permute-start(bf16[256,16,256]{2,1,0:T(8,128)(2,1)} %get-tuple-element.45), channel_id=1, source_target_pairs={{0,3},{1,2},{2,1},{3,0},{4,7},{5,6},{6,5},{7,4}} | collective-permute-start | bytes 6291464 | tf_op jit(solution)/shard_map/ppermute | solution.py:190
  231.9 126.1 %collective-permute-start.10 = (bf16[256,16,256]{2,1,0:T(8,128)(2,1)}, bf16[256,16,256]{2,1,0:T(8,128)(2,1)S(1)}, u32[]{:S(2)}, u32[]{:S(2)}) collective-permute-start(bf16[256,16,256]{2,1,0:T(8,128)(2,1)} %get-tuple-element.53), channel_id=1, source_target_pairs={{0,2},{1,3},{2,0},{3,1},{4,6},{5,7},{6,4},{7,5}} | collective-permute-start | bytes 6291464 | tf_op jit(solution)/shard_map/ppermute | solution.py:190
  233.2 168.0 %collective-permute-start.11 = (bf16[256,16,256]{2,1,0:T(8,128)(2,1)}, bf16[256,16,256]{2,1,0:T(8,128)(2,1)}, u32[]{:S(2)}, u32[]{:S(2)}) collective-permute-start(bf16[256,16,256]{2,1,0:T(8,128)(2,1)} %get-tuple-element.54), channel_id=1, source_target_pairs={{0,3},{1,2},{2,1},{3,0},{4,7},{5,6},{6,5},{7,4}} | collective-permute-start | bytes 6291464 | tf_op jit(solution)/shard_map/ppermute | solution.py:190
  358.0 18.7 %copy-start.2 = (bf16[256,16,256]{2,1,0:T(8,128)(2,1)}, bf16[256,16,256]{2,1,0:T(8,128)(2,1)S(1)}, u32[]{:S(2)}) copy-start(bf16[256,16,256]{2,1,0:T(8,128)(2,1)S(1)} %collective-permute-done.10.refs_9_.refs_2_) | copy-start | bytes 6291460
  358.0 43.3 %collective-permute-start.9 = (bf16[256,16,256]{2,1,0:T(8,128)(2,1)}, bf16[256,16,256]{2,1,0:T(8,128)(2,1)}, u32[]{:S(2)}, u32[]{:S(2)}) collective-permute-start(bf16[256,16,256]{2,1,0:T(8,128)(2,1)} %get-tuple-element.52), channel_id=1, source_target_pairs={{0,1},{1,0},{2,3},{3,2},{4,5},{5,4},{6,7},{7,6}} | collective-permute-start | bytes 6291464 | tf_op jit(solution)/shard_map/ppermute | solution.py:190
  412.0 53.7 %collective-permute-start.12 = (bf16[256,16,256]{2,1,0:T(8,128)(2,1)}, bf16[256,16,256]{2,1,0:T(8,128)(2,1)}, u32[]{:S(2)}, u32[]{:S(2)}) collective-permute-start(bf16[256,16,256]{2,1,0:T(8,128)(2,1)} %get-tuple-element.56), channel_id=1, source_target_pairs={{0,1},{1,0},{2,3},{3,2},{4,5},{5,4},{6,7},{7,6}} | collective-permute-start | bytes 6291464 | tf_op jit(solution)/shard_map/ppermute | solution.py:190
  412.6 55.4 %collective-permute-start.13 = (bf16[256,16,256]{2,1,0:T(8,128)(2,1)}, bf16[256,16,256]{2,1,0:T(8,128)(2,1)}, u32[]{:S(2)}, u32[]{:S(2)}) collective-permute-start(bf16[256,16,256]{2,1,0:T(8,128)(2,1)} %get-tuple-element.57), channel_id=1, source_target_pairs={{0,2},{1,3},{2,0},{3,1},{4,6},{5,7},{6,4},{7,5}} | collective-permute-start | bytes 6291464 | tf_op jit(solution)/shard_map/ppermute | solution.py:190
  414.4 90.9 %collective-permute-start.14 = (bf16[256,16,256]{2,1,0:T(8,128)(2,1)}, bf16[256,16,256]{2,1,0:T(8,128)(2,1)}, u32[]{:S(2)}, u32[]{:S(2)}) collective-permute-start(bf16[256,16,256]{2,1,0:T(8,128)(2,1)} %get-tuple-element.58), channel_id=1, source_target_pairs={{0,3},{1,2},{2,1},{3,0},{4,7},{5,6},{6,5},{7,4}} | collective-permute-start | bytes 6291464 | tf_op jit(solution)/shard_map/ppermute | solution.py:190
  424.9 99.8 %collective-permute-start.15 = (bf16[256,16,256]{2,1,0:T(8,128)(2,1)}, bf16[256,16,256]{2,1,0:T(8,128)(2,1)S(1)}, u32[]{:S(2)}, u32[]{:S(2)}) collective-permute-start(bf16[256,16,256]{2,1,0:T(8,128)(2,1)} %get-tuple-element.65), channel_id=1, source_target_pairs={{0,1},{1,0},{2,3},{3,2},{4,5},{5,4},{6,7},{7,6}} | collective-permute-start | bytes 6291464 | tf_op jit(solution)/shard_map/ppermute | solution.py:190
  425.2 125.8 %collective-permute-start.16 = (bf16[256,16,256]{2,1,0:T(8,128)(2,1)}, bf16[256,16,256]{2,1,0:T(8,128)(2,1)}, u32[]{:S(2)}, u32[]{:S(2)}) collective-permute-start(bf16[256,16,256]{2,1,0:T(8,128)(2,1)} %get-tuple-element.66), channel_id=1, source_target_pairs={{0,2},{1,3},{2,0},{3,1},{4,6},{5,7},{6,4},{7,5}} | collective-permute-start | bytes 6291464 | tf_op jit(solution)/shard_map/ppermute | solution.py:190
  465.7 128.6 %collective-permute-start.17 = (bf16[256,16,256]{2,1,0:T(8,128)(2,1)}, bf16[256,16,256]{2,1,0:T(8,128)(2,1)}, u32[]{:S(2)}, u32[]{:S(2)}) collective-permute-start(bf16[256,16,256]{2,1,0:T(8,128)(2,1)} %get-tuple-element.67), channel_id=1, source_target_pairs={{0,3},{1,2},{2,1},{3,0},{4,7},{5,6},{6,5},{7,4}} | collective-permute-start | bytes 6291464 | tf_op jit(solution)/shard_map/ppermute | solution.py:190
  524.7 69.6 %copy-start.6 = (bf16[256,16,256]{2,1,0:T(8,128)(2,1)}, bf16[256,16,256]{2,1,0:T(8,128)(2,1)S(1)}, u32[]{:S(2)}) copy-start(bf16[256,16,256]{2,1,0:T(8,128)(2,1)S(1)} %collective-permute-done.15.refs_1_) | copy-start | bytes 6291460
  594.3 20.9 %copy-start.4 = (bf16[3,2304]{1,0:T(4,128)(2,1)S(1)}, bf16[3,2304]{1,0:T(4,128)(2,1)}, u32[]{:S(2)}) copy-start(bf16[3,2304]{1,0:T(4,128)(2,1)} %param.12) | copy-start | bytes 41476

commit v2 on v1

v2 whole, which is shorter than its diff:
```python
import functools

import jax
import jax.numpy as jnp
from jax import lax
from jax.experimental import pallas as pl
from jax.experimental.pallas import tpu as pltpu
from jax.sharding import PartitionSpec as P


WINDOW = 4096
THETA = 10000.0
EPS = 1e-5
BLK = 16
CHUNK = 512
CB = CHUNK // BLK
NCH = WINDOW // CHUNK
PLAN = (
    (True, 0, 0, 1), (True, 0, 1, 3), (True, 0, 4, 4), (True, 1, 0, 4), (True, 1, 4, 4), (True, 2, 0, 4), (True, 2, 4, 4),
    (False, 0, 0, 4), (False, 0, 4, 4), (False, 1, 0, 4), (False, 1, 4, 4), (False, 2, 0, 4), (False, 2, 4, 2), (False, 2, 6, 1), (False, 2, 7, 1),
)


def rotate(heads, positions):
    head_dim = heads.shape[-1]
    half_dim = head_dim // 2
    inv_freq = THETA ** (-2.0 * jnp.arange(half_dim, dtype=jnp.float32) / head_dim)
    angles = positions.astype(jnp.float32).reshape(positions.shape + (1,) * (heads.ndim - 1)) * inv_freq
    cos_part = jnp.cos(angles)
    sin_part = jnp.sin(angles)
    first_half = heads[..., :half_dim].astype(jnp.float32)
    second_half = heads[..., half_dim:].astype(jnp.float32)
    return jnp.concatenate([first_half * cos_part - second_half * sin_part, second_half * cos_part + first_half * sin_part], axis=-1).astype(jnp.bfloat16)


def blank(shape, dtype):
    return pl.pallas_call(
        lambda o_ref: None,
        out_shape=jax.ShapeDtypeStruct(shape, dtype),
        out_specs=pl.BlockSpec(memory_space=pl.ANY),
        name="blank",
    )()


def pick_kernel(ways, first, n_ref, r_ref, *refs):
    x_refs, y_refs, o_refs = refs[:ways], refs[ways:2 * ways], refs[-ways:]
    c = first + pl.program_id(0)
    s0 = c * CHUNK
    for d in range(ways):
        n = n_ref[d]
        lap, m = n // WINDOW, lax.rem(n, WINDOW)
        cb = m // CHUNK

        @pl.when((c != cb) & ((c < cb) | (lap >= 1)))
        def _():
            o_refs[d][...] = x_refs[d][0]

        @pl.when((c > cb) & (lap == 0))
        def _():
            o_refs[d][...] = jnp.zeros(o_refs[d].shape, o_refs[d].dtype)

        @pl.when(c == cb)
        def _():
            shape = (CB, BLK, 256)
            slots = s0 + BLK * lax.broadcasted_iota(jnp.int32, shape, 0) + lax.broadcasted_iota(jnp.int32, shape, 1)
            old = jnp.where(lap >= 1, y_refs[d][0].astype(jnp.float32), 0.0)
            o_refs[d][...] = jnp.where(slots < m, x_refs[d][0].astype(jnp.float32), old).astype(jnp.bfloat16)


def pick(prefill, lens, rows, first, count):
    ways = rows.shape[0]
    seq_blocks = prefill.shape[1]

    def x_map(d):
        def index(i, n_ref, r_ref):
            c, n = first + i, n_ref[d]
            lap, m = n // WINDOW, lax.rem(n, WINDOW)
            from_lap = jnp.where(c <= m // CHUNK, lap, jnp.maximum(lap - 1, 0))
            return r_ref[d], jnp.minimum(from_lap * NCH + c, seq_blocks // CB - 1), 0, 0

        return pl.BlockSpec((1, CB, BLK, 256), index)

    def y_map(d):
        def index(i, n_ref, r_ref):
            n = n_ref[d]
            lap, m = n // WINDOW, lax.rem(n, WINDOW)
            return r_ref[d], jnp.maximum(lap - 1, 0) * NCH + m // CHUNK, 0, 0

        return pl.BlockSpec((1, CB, BLK, 256), index)

    return pl.pallas_call(
        functools.partial(pick_kernel, ways, first),
        grid_spec=pltpu.PrefetchScalarGridSpec(
            num_scalar_prefetch=2,
            grid=(count,),
            in_specs=[x_map(d) for d in range(ways)] + [y_map(d) for d in range(ways)],
            out_specs=[pl.BlockSpec((CB, BLK, 256), lambda i, n_ref, r_ref: (i, 0, 0))] * ways,
        ),
        out_shape=[jax.ShapeDtypeStruct((count * CB, BLK, 256), prefill.dtype)] * ways,
        compiler_params=pltpu.CompilerParams(dimension_semantics=("arbitrary",), vmem_limit_bytes=67_043_328),
        cost_estimate=pl.CostEstimate(flops=10_000_000, bytes_accessed=count * 4_000_000, transcendentals=0),
        name="pick",
    )(lens, rows, *([prefill] * (2 * ways)))


def assemble_kernel(is_key, ways, first, count, n_ref, me_ref, *refs):
    x_refs = refs[:ways]
    new_ref, qp_ref, prev_ref, _, _, cache_ref, res_ref, acc, mix = refs[ways:ways + 9]
    i = pl.program_id(0)
    s0 = (first + i) * CHUNK
    me = me_ref[0]
    n = n_ref[0]
    lap, m = n // WINDOW, lax.rem(n, WINDOW)

    @pl.when((s0 <= m) & (m < s0 + CHUNK))
    def _():
        b = (m - s0) // BLK
        here = lax.broadcasted_iota(jnp.int32, (BLK, 256), 0) == lax.rem(m, BLK)
        for d in range(ways):
            new = jnp.broadcast_to(new_ref[me ^ d], (BLK, 256))
            x_refs[d][b] = jnp.where(here, new, x_refs[d][b].astype(jnp.float32)).astype(jnp.bfloat16)

    xs = [x_refs[d][...].reshape(CHUNK, 256) for d in range(ways)]
    if is_key:
        cols = s0 + lax.broadcasted_iota(jnp.int32, (8, CHUNK), 1)
        live = (lap >= 1) | (cols <= n)
        for d in range(ways):
            s = lax.dot_general(qp_ref[me ^ d], xs[d], (((1,), (1,)), ((), ())), preferred_element_type=jnp.float32)
            res_ref[me ^ d] = jnp.where(live, s / 16.0, -jnp.inf)
    else:
        @pl.when(i == 0)
        def _():
            acc[...] = prev_ref[...]

        for d in range(ways):
            acc[me ^ d] += jnp.dot(qp_ref[me ^ d], xs[d], preferred_element_type=jnp.float32)

        @pl.when(i == count - 1)
        def _():
            res_ref[...] = acc[...]

    for d in range(ways):
        x = xs[d].astype(jnp.float32)
        for half in range(2):
            mix[half, pl.ds(me ^ d, CHUNK, stride=ways), :] = x[:, half * 128:(half + 1) * 128]
    joined = jnp.concatenate([mix[half].astype(jnp.bfloat16) for half in range(2)], axis=1)
    cache_ref[0] = joined.reshape(CHUNK, ways, 256)


def assemble(is_key, row, first, n, me, parts, new, qp, prev, cache, after):
    ways = len(parts)
    count = parts[0].shape[0] // CB
    whole = lambda *shape: pl.BlockSpec(shape, lambda i, n_ref, me_ref: (0,) * len(shape))
    by_chunk = pl.BlockSpec((ways, 8, CHUNK), lambda i, n_ref, me_ref: (0, 0, first + i))
    anywhere = pl.BlockSpec(memory_space=pl.ANY)
    if is_key:
        qp_spec, prev_spec, res_spec = whole(ways, 8, 256), anywhere, by_chunk
    else:
        qp_spec, prev_spec, res_spec = by_chunk, whole(ways, 8, 256), whole(ways, 8, 256)
    aliases = {2 + ways + 3: 0}
    if is_key:
        aliases[2 + ways + 2] = 1
    return pl.pallas_call(
        functools.partial(assemble_kernel, is_key, ways, first, count),
        grid_spec=pltpu.PrefetchScalarGridSpec(
            num_scalar_prefetch=2,
            grid=(count,),
            in_specs=[pl.BlockSpec((CB, BLK, 256), lambda i, n_ref, me_ref: (i, 0, 0))] * ways + [whole(ways, 1, 256), qp_spec, prev_spec, anywhere, anywhere],
            out_specs=[pl.BlockSpec((1, CHUNK, ways, 256), lambda i, n_ref, me_ref: (row, first + i, 0, 0)), res_spec],
            scratch_shapes=[pltpu.VMEM((ways, 8, 256), jnp.float32), pltpu.VMEM((2, ways * CHUNK, 128), jnp.float32)],
        ),
        out_shape=[jax.ShapeDtypeStruct(cache.shape, cache.dtype), jax.ShapeDtypeStruct(prev.shape, prev.dtype)],
        input_output_aliases=aliases,
        compiler_params=pltpu.CompilerParams(dimension_semantics=("arbitrary",), vmem_limit_bytes=67_043_328),
        cost_estimate=pl.CostEstimate(flops=10_000_000, bytes_accessed=count * 4_000_000, transcendentals=0),
        name="assemble_keys" if is_key else "assemble_values",
    )(n, me, *parts, new, qp, prev, cache, after)


def solution(mesh):
    head_spec = P('dp', None, 'sh', None)
    row_spec = P(('dp', 'sh'))
    full_spec = P(None, None)
    ways = mesh.shape['sh']

    def step(k_prefill, v_prefill, lengths, residual, norm_gain, w_query, w_key, w_value, w_out):
        num_rows = residual.shape[0]
        all_rows, seq = k_prefill.shape[0], k_prefill.shape[1]
        heads = ways
        me = lax.axis_index('sh').astype(jnp.int32)
        my_lengths = lax.dynamic_slice_in_dim(lengths, me * num_rows, num_rows)
        peers = me ^ jnp.arange(ways, dtype=jnp.int32)
        k_blocks = k_prefill.reshape(all_rows, seq // BLK, BLK, 256)
        v_blocks = v_prefill.reshape(all_rows, seq // BLK, BLK, 256)

        stages = []
        for is_key, r, first, count in PLAN:
            rows = peers * num_rows + r
            sent = pick(k_blocks if is_key else v_blocks, lengths[rows], rows, first, count)
            got = [sent[0]]
            for d in range(1, ways):
                got.append(lax.ppermute(sent[d], 'sh', [(i, i ^ d) for i in range(ways)]))
            stages.append(got)
        last_sent = sent[0]

        resid_f32 = residual.astype(jnp.float32)
        inv_rms = lax.rsqrt(jnp.mean(resid_f32 * resid_f32, axis=-1, keepdims=True) + EPS)
        normed = (resid_f32 * inv_rms * norm_gain.astype(jnp.float32)).astype(jnp.bfloat16)
        q_group = w_query.shape[1] // (heads * 256)
        q_heads = jnp.dot(normed, w_query, preferred_element_type=jnp.float32).astype(jnp.bfloat16).reshape(num_rows, heads, q_group, 256)
        k_new = jnp.dot(normed, w_key, preferred_element_type=jnp.float32).astype(jnp.bfloat16).reshape(num_rows, heads, 256)
        v_new = jnp.dot(normed, w_value, preferred_element_type=jnp.float32).astype(jnp.bfloat16).reshape(num_rows, heads, 256)
        q_heads = rotate(q_heads, my_lengths)
        k_new = rotate(k_new, my_lengths)
        k_new, v_new = k_new.astype(jnp.float32)[:, :, None], v_new.astype(jnp.float32)[:, :, None]
        q_pad = jnp.pad(q_heads, ((0, 0), (0, 0), (0, 8 - q_group), (0, 0)))

        me1 = me.reshape(1)
        cache_shape = (num_rows, WINDOW, heads, 256)
        k_cache, v_cache = blank(cache_shape, jnp.bfloat16), blank(cache_shape, jnp.bfloat16)
        scores = [blank((heads, 8, WINDOW), jnp.float32) for _ in range(num_rows)]
        sums = [jnp.zeros((heads, 8, 256), jnp.float32) for _ in range(num_rows)]
        weights = [None] * num_rows
        for (is_key, r, first, count), got in zip(PLAN, stages):
            if is_key:
                k_cache, scores[r] = assemble(True, r, first, my_lengths[r:r + 1], me1, got, k_new[r], q_pad[r], scores[r], k_cache, last_sent)
                if first + count == NCH:
                    exp_scores = jnp.exp(scores[r] - jnp.max(scores[r], axis=-1, keepdims=True))
                    weights[r] = (exp_scores / jnp.sum(exp_scores, axis=-1, keepdims=True)).astype(jnp.bfloat16)
            else:
                v_cache, sums[r] = assemble(False, r, first, my_lengths[r:r + 1], me1, got, v_new[r], weights[r], sums[r], v_cache, last_sent)
        attn = [x[:, :q_group].astype(jnp.bfloat16).reshape(1, heads * q_group * 256) for x in sums]
        attn_out = jnp.concatenate(attn, axis=0)
        resid_out = (resid_f32 + jnp.dot(attn_out, w_out, preferred_element_type=jnp.float32)).astype(jnp.bfloat16)
        return resid_out, k_cache, v_cache

    return jax.shard_map(step, mesh=mesh, in_specs=(head_spec, head_spec, P('dp'), P(('dp', 'sh'), None), P(None), full_spec, full_spec, full_spec, full_spec), out_specs=(P(('dp', 'sh'), None), row_spec, row_spec), check_vma=False)
```

time: 623 us -> 618 us (level)
  waiting for transfers between devices: 395 us -> 363 us
  starting transfers between devices: 14.2 us -> 34.4 us
  other arithmetic: 9.57 us -> 16.9 us
    ppermute x18 -> x45, waiting for transfers between devices: 395 us -> 363 us  [step(): got.append(lax.ppermute(sent[d], 'sh', [(i, i ^ d) for i in range(ways)]))]
    ppermute x18 -> x45, starting transfers between devices: 14.2 us -> 34.4 us  [step(): got.append(lax.ppermute(sent[d], 'sh', [(i, i ^ d) for i in range(ways)]))]
    pallas_call x12 -> x30, Pallas kernels: 176 us -> 170 us  [the longest x15 88.3 us: assemble(): pl.pallas_call(functools.partial(assemble_kernel, is_key, ways, first, co...]
  transfers between devices with their start and end apart: 18 -> 45, of which waited for: 7 -> 21; matrix products, arithmetic and copies ran while one was open for 4% -> 6% of each run, Pallas kernels for 24% -> 26%
where the time goes in v2:
time: 618 us; the launch traced here: 615 us
  waiting for transfers between devices  363 us (59%)
  Pallas kernels  170 us (28%)
  starting transfers between devices  34.4 us (6%)
  other arithmetic  16.9 us (3%)
  matrix products  16.9 us (3%)
  local copies, waits for them, and re-layouts  13 us (2%)
    ppermute x45, waiting for transfers between devices, step(): got.append(lax.ppermute(sent[d], 'sh', [(i, i ^ d) for i in range(ways)]))  363 us
    pallas_call x15, Pallas kernels, assemble(): pl.pallas_call(functools.partial(assemble_kernel, is_key, ways, first, co...  88.3 us
    pallas_call x15, Pallas kernels, pick(): pl.pallas_call(functools.partial(pick_kernel, ways, first), grid_spec=plt...  82 us
    ppermute x45, starting transfers between devices, step(): got.append(lax.ppermute(sent[d], 'sh', [(i, i ^ d) for i in range(ways)]))  34.4 us
  transfers between devices with their start and end apart: 45, of which 21 were waited for; matrix products, arithmetic and copies ran while one was open for 6% of the time, Pallas kernels for 26%

profile of v2, /device:TPU:0, one launch (start us, length us, event | category | flops | bytes accessed | tf_op | source)
XLA Modules:
  0.0 615.4 jit_solution(16291927582955597188)
XLA Ops:
  3.5 4.0 pick.28
  17.7 3.5 pick.27
  21.6 5.9 pick.17
  33.7 6.1 pick.16
  39.8 6.0 pick.20
  45.9 33.1 %collective-permute-done.40.refs_2_ = bf16[64,16,256]{2,1,0:T(8,128)(2,1)} collective-permute-done((bf16[64,16,256]{2,1,0:T(8,128)(2,1)}, bf16[64,16,256]{2,1,0:T(8,128)(2,1)}, u32[]{:S(2)}, u32[]{:S(2)}) %collective-permute-start.40) | collective-permute-done | bytes 524320 | tf_op jit(solution)/shard_map/ppermute | solution.py:202
  79.0 9.5 %collective-permute-done.41.refs_3_ = bf16[64,16,256]{2,1,0:T(8,128)(2,1)} collective-permute-done((bf16[64,16,256]{2,1,0:T(8,128)(2,1)}, bf16[64,16,256]{2,1,0:T(8,128)(2,1)}, u32[]{:S(2)}, u32[]{:S(2)}) %collective-permute-start.41) | collective-permute-done | bytes 524320 | tf_op jit(solution)/shard_map/ppermute | solution.py:202
  94.3 6.1 pick.15
  100.4 6.3 %pick.23 = (bf16[128,16,256]{2,1,0:T(8,128)(2,1)}, bf16[128,16,256]{2,1,0:T(8,128)(2,1)}, bf16[128,16,256]{2,1,0:T(8,128)(2,1)}, bf16[128,16,256]{2,1,0:T(8,128)(2,1)}) custom-call(s32[4]{0:T(128)} %gather_fusion.2, s32[4]{0:T(128)} %get-tuple-element.206.r_ref, bf16[12,640,16,256]{3,2,1,0:T(8,128)(2,1)} %bitcast.123, bf16[12,640,16,256]{3,2,1,0:T(8,128)(2,1)} %bitcast.121, ...), custom_call_target="tpu_custom_call" | custom-call | flops 10000000 | bytes 16000000 | tf_op jit(solution)/shard_map/pick/pallas_call | solution.py:91
  106.9 8.0 %collective-permute-done.4.refs_2_ = bf16[128,16,256]{2,1,0:T(8,128)(2,1)} collective-permute-done((bf16[128,16,256]{2,1,0:T(8,128)(2,1)}, bf16[128,16,256]{2,1,0:T(8,128)(2,1)}, u32[]{:S(2)}, u32[]{:S(2)}) %collective-permute-start.4) | collective-permute-done | bytes 1048608 | tf_op jit(solution)/shard_map/ppermute | solution.py:202
  114.9 21.8 %collective-permute-done.5.refs_3_ = bf16[128,16,256]{2,1,0:T(8,128)(2,1)} collective-permute-done((bf16[128,16,256]{2,1,0:T(8,128)(2,1)}, bf16[128,16,256]{2,1,0:T(8,128)(2,1)}, u32[]{:S(2)}, u32[]{:S(2)}) %collective-permute-start.5) | collective-permute-done | bytes 1048608 | tf_op jit(solution)/shard_map/ppermute | solution.py:202
  138.6 21.2 %collective-permute-done.13.refs_2_ = bf16[128,16,256]{2,1,0:T(8,128)(2,1)} collective-permute-done((bf16[128,16,256]{2,1,0:T(8,128)(2,1)}, bf16[128,16,256]{2,1,0:T(8,128)(2,1)}, u32[]{:S(2)}, u32[]{:S(2)}) %collective-permute-start.13) | collective-permute-done | bytes 1048608 | tf_op jit(solution)/shard_map/ppermute | solution.py:202
  159.8 6.0 pick.22
  165.8 15.9 %collective-permute-done.14.refs_3_ = bf16[128,16,256]{2,1,0:T(8,128)(2,1)} collective-permute-done((bf16[128,16,256]{2,1,0:T(8,128)(2,1)}, bf16[128,16,256]{2,1,0:T(8,128)(2,1)}, u32[]{:S(2)}, u32[]{:S(2)}) %collective-permute-start.14) | collective-permute-done | bytes 1048608 | tf_op jit(solution)/shard_map/ppermute | solution.py:202
  183.5 21.2 %collective-permute-done.1.refs_2_ = bf16[128,16,256]{2,1,0:T(8,128)(2,1)} collective-permute-done((bf16[128,16,256]{2,1,0:T(8,128)(2,1)}, bf16[128,16,256]{2,1,0:T(8,128)(2,1)}, u32[]{:S(2)}, u32[]{:S(2)}) %collective-permute-start.1) | collective-permute-done | bytes 1048608 | tf_op jit(solution)/shard_map/ppermute | solution.py:202
  204.8 21.8 %collective-permute-done.2.refs_3_ = bf16[128,16,256]{2,1,0:T(8,128)(2,1)} collective-permute-done((bf16[128,16,256]{2,1,0:T(8,128)(2,1)}, bf16[128,16,256]{2,1,0:T(8,128)(2,1)}, u32[]{:S(2)}, u32[]{:S(2)}) %collective-permute-start.2) | collective-permute-done | bytes 1048608 | tf_op jit(solution)/shard_map/ppermute | solution.py:202
  228.5 6.4 %pick.24 = (bf16[128,16,256]{2,1,0:T(8,128)(2,1)}, bf16[128,16,256]{2,1,0:T(8,128)(2,1)}, bf16[128,16,256]{2,1,0:T(8,128)(2,1)}, bf16[128,16,256]{2,1,0:T(8,128)(2,1)}) custom-call(s32[4]{0:T(128)} %gather_fusion.2, s32[4]{0:T(128)} %get-tuple-element.206.r_ref, bf16[12,640,16,256]{3,2,1,0:T(8,128)(2,1)} %bitcast.64, bf16[12,640,16,256]{3,2,1,0:T(8,128)(2,1)} %bitcast.65, ...), custom_call_target="tpu_custom_call" | custom-call | flops 10000000 | bytes 16000000 | tf_op jit(solution)/shard_map/pick/pallas_call | solution.py:91
  234.9 6.0 pick.21
  240.8 8.9 %collective-permute-done.22.refs_2_ = bf16[128,16,256]{2,1,0:T(8,128)(2,1)} collective-permute-done((bf16[128,16,256]{2,1,0:T(8,128)(2,1)}, bf16[128,16,256]{2,1,0:T(8,128)(2,1)}, u32[]{:S(2)}, u32[]{:S(2)}) %collective-permute-start.22) | collective-permute-done | bytes 1048608 | tf_op jit(solution)/shard_map/ppermute | solution.py:202
  249.7 21.8 %collective-permute-done.23.refs_3_ = bf16[128,16,256]{2,1,0:T(8,128)(2,1)} collective-permute-done((bf16[128,16,256]{2,1,0:T(8,128)(2,1)}, bf16[128,16,256]{2,1,0:T(8,128)(2,1)}, u32[]{:S(2)}, u32[]{:S(2)}) %collective-permute-start.23) | collective-permute-done | bytes 1048608 | tf_op jit(solution)/shard_map/ppermute | solution.py:202
  273.4 21.2 %collective-permute-done.19.refs_2_ = bf16[128,16,256]{2,1,0:T(8,128)(2,1)} collective-permute-done((bf16[128,16,256]{2,1,0:T(8,128)(2,1)}, bf16[128,16,256]{2,1,0:T(8,128)(2,1)}, u32[]{:S(2)}, u32[]{:S(2)}) %collective-permute-start.19) | collective-permute-done | bytes 1048608 | tf_op jit(solution)/shard_map/ppermute | solution.py:202
  294.7 21.8 %collective-permute-done.20.refs_3_ = bf16[128,16,256]{2,1,0:T(8,128)(2,1)} collective-permute-done((bf16[128,16,256]{2,1,0:T(8,128)(2,1)}, bf16[128,16,256]{2,1,0:T(8,128)(2,1)}, u32[]{:S(2)}, u32[]{:S(2)}) %collective-permute-start.20) | collective-permute-done | bytes 1048608 | tf_op jit(solution)/shard_map/ppermute | solution.py:202
  319.8 6.4 %pick.26 = (bf16[128,16,256]{2,1,0:T(8,128)(2,1)}, bf16[128,16,256]{2,1,0:T(8,128)(2,1)}, bf16[128,16,256]{2,1,0:T(8,128)(2,1)}, bf16[128,16,256]{2,1,0:T(8,128)(2,1)}) custom-call(s32[4]{0:T(128)} %gather_fusion.1, s32[4]{0:T(128)} %broadcast_add_fusion.1.r_ref, bf16[12,640,16,256]{3,2,1,0:T(8,128)(2,1)} %bitcast.136, bf16[12,640,16,256]{3,2,1,0:T(8,128)(2,1)} %bitcast.137, ...), custom_call_target="tpu_custom_call" | custom-call | flops 10000000 | bytes 16000000 | tf_op jit(solution)/shard_map/pick/pallas_call | solution.py:91
  326.2 6.1 pick.25
  335.1 5.1 convolution_convert_fusion
  340.8 20.6 %collective-permute-done.26.refs_3_ = bf16[128,16,256]{2,1,0:T(8,128)(2,1)} collective-permute-done((bf16[128,16,256]{2,1,0:T(8,128)(2,1)}, bf16[128,16,256]{2,1,0:T(8,128)(2,1)}, u32[]{:S(2)}, u32[]{:S(2)}) %collective-permute-start.26) | collective-permute-done | bytes 1048608 | tf_op jit(solution)/shard_map/ppermute | solution.py:202
  363.3 21.2 %collective-permute-done.16.refs_2_ = bf16[128,16,256]{2,1,0:T(8,128)(2,1)} collective-permute-done((bf16[128,16,256]{2,1,0:T(8,128)(2,1)}, bf16[128,16,256]{2,1,0:T(8,128)(2,1)}, u32[]{:S(2)}, u32[]{:S(2)}) %collective-permute-start.16) | collective-permute-done | bytes 1048608 | tf_op jit(solution)/shard_map/ppermute | solution.py:202
  386.5 6.6 %pick.29 = (bf16[128,16,256]{2,1,0:T(8,128)(2,1)}, bf16[128,16,256]{2,1,0:T(8,128)(2,1)}, bf16[128,16,256]{2,1,0:T(8,128)(2,1)}, bf16[128,16,256]{2,1,0:T(8,128)(2,1)}) custom-call(s32[4]{0:T(128)} %gather_fusion.1, s32[4]{0:T(128)} %broadcast_add_fusion.1.r_ref, bf16[12,640,16,256]{3,2,1,0:T(8,128)(2,1)} %bitcast.80, bf16[12,640,16,256]{3,2,1,0:T(8,128)(2,1)} %bitcast.81, ...), custom_call_target="tpu_custom_call" | custom-call | flops 10000000 | bytes 16000000 | tf_op jit(solution)/shard_map/pick/pallas_call | solution.py:91
  398.9 7.5 %collective-permute-done.17.refs_3_ = bf16[128,16,256]{2,1,0:T(8,128)(2,1)} collective-permute-done((bf16[128,16,256]{2,1,0:T(8,128)(2,1)}, bf16[128,16,256]{2,1,0:T(8,128)(2,1)}, u32[]{:S(2)}, u32[]{:S(2)}) %collective-permute-start.17) | collective-permute-done | bytes 1048608 | tf_op jit(solution)/shard_map/ppermute | solution.py:202
  408.2 21.2 %collective-permute-done.34.refs_2_ = bf16[128,16,256]{2,1,0:T(8,128)(2,1)} collective-permute-done((bf16[128,16,256]{2,1,0:T(8,128)(2,1)}, bf16[128,16,256]{2,1,0:T(8,128)(2,1)}, u32[]{:S(2)}, u32[]{:S(2)}) %collective-permute-start.34) | collective-permute-done | bytes 1048608 | tf_op jit(solution)/shard_map/ppermute | solution.py:202
  429.5 21.8 %collective-permute-done.35.refs_3_ = bf16[128,16,256]{2,1,0:T(8,128)(2,1)} collective-permute-done((bf16[128,16,256]{2,1,0:T(8,128)(2,1)}, bf16[128,16,256]{2,1,0:T(8,128)(2,1)}, u32[]{:S(2)}, u32[]{:S(2)}) %collective-permute-start.35) | collective-permute-done | bytes 1048608 | tf_op jit(solution)/shard_map/ppermute | solution.py:202
  463.1 3.5 assemble_keys.7
  466.5 5.8 assemble_keys.8
  472.3 6.6 %assemble_keys.9 = (bf16[3,4096,4,256]{3,2,1,0:T(4,128)(2,1)}, f32[4,8,4096]{2,1,0:T(8,128)}) custom-call(s32[1]{0:T(128)} %get-tuple-element.200.n_ref, s32[1]{0:T(128)} %bitcast.me_ref, bf16[128,16,256]{2,1,0:T(8,128)(2,1)} %get-tuple-element.97.refs_0_, ...), custom_call_target="tpu_custom_call", output_to_operand_aliasing={{0}: (9, {}), {1}: (8, {})} | custom-call | flops 10000000 | bytes 16000000 | tf_op jit(solution)/shard_map/assemble_keys/pallas_call | solution.py:163
  478.9 6.6 %assemble_keys.10 = (bf16[3,4096,4,256]{3,2,1,0:T(4,128)(2,1)}, f32[4,8,4096]{2,1,0:T(8,128)}) custom-call(s32[1]{0:T(128)} %get-tuple-element.201.n_ref, s32[1]{0:T(128)} %bitcast.me_ref, bf16[128,16,256]{2,1,0:T(8,128)(2,1)} %get-tuple-element.130.refs_0_, ...), custom_call_target="tpu_custom_call", output_to_operand_aliasing={{0}: (9, {}), {1}: (8, {})} | custom-call | flops 10000000 | bytes 16000000 | tf_op jit(solution)/shard_map/assemble_keys/pallas_call | solution.py:163
  485.4 6.5 %assemble_keys.11 = (bf16[3,4096,4,256]{3,2,1,0:T(4,128)(2,1)}, f32[4,8,4096]{2,1,0:T(8,128)}) custom-call(s32[1]{0:T(128)} %get-tuple-element.201.n_ref, s32[1]{0:T(128)} %bitcast.me_ref, bf16[128,16,256]{2,1,0:T(8,128)(2,1)} %get-tuple-element.126.refs_0_, ...), custom_call_target="tpu_custom_call", output_to_operand_aliasing={{0}: (9, {}), {1}: (8, {})} | custom-call | flops 10000000 | bytes 16000000 | tf_op jit(solution)/shard_map/assemble_keys/pallas_call | solution.py:163
  498.1 21.2 %collective-permute-done.43.refs_2_ = bf16[128,16,256]{2,1,0:T(8,128)(2,1)} collective-permute-done((bf16[128,16,256]{2,1,0:T(8,128)(2,1)}, bf16[128,16,256]{2,1,0:T(8,128)(2,1)}, u32[]{:S(2)}, u32[]{:S(2)}) %collective-permute-start.43) | collective-permute-done | bytes 1048608 | tf_op jit(solution)/shard_map/ppermute | solution.py:202
  521.2 20.0 %collective-permute-done.44.refs_3_ = bf16[128,16,256]{2,1,0:T(8,128)(2,1)} collective-permute-done((bf16[128,16,256]{2,1,0:T(8,128)(2,1)}, bf16[128,16,256]{2,1,0:T(8,128)(2,1)}, u32[]{:S(2)}, u32[]{:S(2)}) %collective-permute-start.44) | collective-permute-done | bytes 1048608 | tf_op jit(solution)/shard_map/ppermute | solution.py:202
  545.9 6.9 %assemble_values.8 = (bf16[3,4096,4,256]{3,2,1,0:T(4,128)(2,1)}, f32[4,8,256]{2,1,0:T(8,128)}) custom-call(s32[1]{0:T(128)} %get-tuple-element.200.n_ref, s32[1]{0:T(128)} %bitcast.me_ref, bf16[128,16,256]{2,1,0:T(8,128)(2,1)} %get-tuple-element.115.refs_0_, bf16[128,16,256]{2,1,0:T(8,128)(2,1)} %collective-permute-done.12.refs_1_, ...), custom_call_target="tpu_custom_call", output_to_operand_aliasing={{0}: (9, {})} | custom-call | flops 10000000 | bytes 16000000 | tf_op jit(solution)/shard_map/assemble_values/pallas_call | solution.py:163
  552.8 6.9 %assemble_values.9 = (bf16[3,4096,4,256]{3,2,1,0:T(4,128)(2,1)}, f32[4,8,256]{2,1,0:T(8,128)}) custom-call(s32[1]{0:T(128)} %get-tuple-element.200.n_ref, s32[1]{0:T(128)} %bitcast.me_ref, bf16[128,16,256]{2,1,0:T(8,128)(2,1)} %get-tuple-element.93.refs_0_, bf16[128,16,256]{2,1,0:T(8,128)(2,1)} %collective-permute-done.refs_1_, ...), custom_call_target="tpu_custom_call", output_to_operand_aliasing={{0}: (9, {})} | custom-call | flops 10000000 | bytes 16000000 | tf_op jit(solution)/shard_map/assemble_values/pallas_call | solution.py:163
  559.7 6.9 %assemble_values.10 = (bf16[3,4096,4,256]{3,2,1,0:T(4,128)(2,1)}, f32[4,8,256]{2,1,0:T(8,128)}) custom-call(s32[1]{0:T(128)} %get-tuple-element.201.n_ref, s32[1]{0:T(128)} %bitcast.me_ref, bf16[128,16,256]{2,1,0:T(8,128)(2,1)} %get-tuple-element.138.refs_0_, bf16[128,16,256]{2,1,0:T(8,128)(2,1)} %collective-permute-done.24.refs_1_, ...), custom_call_target="tpu_custom_call", output_to_operand_aliasing={{0}: (9, {})} | custom-call | flops 10000000 | bytes 16000000 | tf_op jit(solution)/shard_map/assemble_values/pallas_call | solution.py:163
  566.6 6.9 %assemble_values.11 = (bf16[3,4096,4,256]{3,2,1,0:T(4,128)(2,1)}, f32[4,8,256]{2,1,0:T(8,128)}) custom-call(s32[1]{0:T(128)} %get-tuple-element.201.n_ref, s32[1]{0:T(128)} %bitcast.me_ref, bf16[128,16,256]{2,1,0:T(8,128)(2,1)} %get-tuple-element.122.refs_0_, bf16[128,16,256]{2,1,0:T(8,128)(2,1)} %collective-permute-done.15.refs_1_, ...), custom_call_target="tpu_custom_call", output_to_operand_aliasing={{0}: (9, {})} | custom-call | flops 10000000 | bytes 16000000 | tf_op jit(solution)/shard_map/assemble_values/pallas_call | solution.py:163
  573.6 6.6 %assemble_keys.12 = (bf16[3,4096,4,256]{3,2,1,0:T(4,128)(2,1)}, f32[4,8,4096]{2,1,0:T(8,128)}) custom-call(s32[1]{0:T(128)} %get-tuple-element.202.n_ref, s32[1]{0:T(128)} %bitcast.me_ref, bf16[128,16,256]{2,1,0:T(8,128)(2,1)} %get-tuple-element.153.refs_0_, ...), custom_call_target="tpu_custom_call", output_to_operand_aliasing={{0}: (9, {}), {1}: (8, {})} | custom-call | flops 10000000 | bytes 16000000 | tf_op jit(solution)/shard_map/assemble_keys/pallas_call | solution.py:163
  580.2 6.6 %assemble_keys.13 = (bf16[3,4096,4,256]{3,2,1,0:T(4,128)(2,1)}, f32[4,8,4096]{2,1,0:T(8,128)}) custom-call(s32[1]{0:T(128)} %get-tuple-element.202.n_ref, s32[1]{0:T(128)} %bitcast.me_ref, bf16[128,16,256]{2,1,0:T(8,128)(2,1)} %get-tuple-element.149.refs_0_, ...), custom_call_target="tpu_custom_call", output_to_operand_aliasing={{0}: (9, {}), {1}: (8, {})} | custom-call | flops 10000000 | bytes 16000000 | tf_op jit(solution)/shard_map/assemble_keys/pallas_call | solution.py:163
  589.0 7.0 %assemble_values.12 = (bf16[3,4096,4,256]{3,2,1,0:T(4,128)(2,1)}, f32[4,8,256]{2,1,0:T(8,128)}) custom-call(s32[1]{0:T(128)} %get-tuple-element.202.n_ref, s32[1]{0:T(128)} %bitcast.me_ref, bf16[128,16,256]{2,1,0:T(8,128)(2,1)} %get-tuple-element.169.refs_0_, bf16[128,16,256]{2,1,0:T(8,128)(2,1)} %collective-permute-done.42.refs_1_, ...), custom_call_target="tpu_custom_call", output_to_operand_aliasing={{0}: (9, {})} | custom-call | flops 10000000 | bytes 16000000 | tf_op jit(solution)/shard_map/assemble_values/pallas_call | solution.py:163
  596.0 4.6 assemble_values.13
  600.6 3.4 assemble_values.14
  609.8 5.6 fusion.18
  (117 shorter events, 83.7 us)
Async XLA Ops:
  7.5 25.8 %collective-permute-start.39 = (bf16[64,16,256]{2,1,0:T(8,128)(2,1)}, bf16[64,16,256]{2,1,0:T(8,128)(2,1)}, u32[]{:S(2)}, u32[]{:S(2)}) collective-permute-start(bf16[64,16,256]{2,1,0:T(8,128)(2,1)} %get-tuple-element.166), channel_id=1, source_target_pairs={{0,1},{1,0},{2,3},{3,2},{4,5},{5,4},{6,7},{7,6}} | collective-permute-start | bytes 1572872 | tf_op jit(solution)/shard_map/ppermute | solution.py:202
  14.7 12.7 %collective-permute-start.10 = (bf16[32,16,256]{2,1,0:T(8,128)(2,1)}, bf16[32,16,256]{2,1,0:T(8,128)(2,1)}, u32[]{:S(2)}, u32[]{:S(2)}) collective-permute-start(bf16[32,16,256]{2,1,0:T(8,128)(2,1)} %get-tuple-element.107), channel_id=1, source_target_pairs={{0,2},{1,3},{2,0},{3,1},{4,6},{5,7},{6,4},{7,5}} | collective-permute-start | bytes 786440 | tf_op jit(solution)/shard_map/ppermute | solution.py:202
  17.5 12.7 %collective-permute-start.11 = (bf16[32,16,256]{2,1,0:T(8,128)(2,1)}, bf16[32,16,256]{2,1,0:T(8,128)(2,1)}, u32[]{:S(2)}, u32[]{:S(2)}) collective-permute-start(bf16[32,16,256]{2,1,0:T(8,128)(2,1)} %get-tuple-element.108), channel_id=1, source_target_pairs={{0,3},{1,2},{2,1},{3,0},{4,7},{5,6},{6,5},{7,4}} | collective-permute-start | bytes 786440 | tf_op jit(solution)/shard_map/ppermute | solution.py:202
  17.6 14.1 %collective-permute-start.9 = (bf16[32,16,256]{2,1,0:T(8,128)(2,1)}, bf16[32,16,256]{2,1,0:T(8,128)(2,1)}, u32[]{:S(2)}, u32[]{:S(2)}) collective-permute-start(bf16[32,16,256]{2,1,0:T(8,128)(2,1)} %get-tuple-element.106), channel_id=1, source_target_pairs={{0,1},{1,0},{2,3},{3,2},{4,5},{5,4},{6,7},{7,6}} | collective-permute-start | bytes 786440 | tf_op jit(solution)/shard_map/ppermute | solution.py:202
  21.2 10.5 %collective-permute-start.36 = (bf16[32,16,256]{2,1,0:T(8,128)(2,1)}, bf16[32,16,256]{2,1,0:T(8,128)(2,1)}, u32[]{:S(2)}, u32[]{:S(2)}) collective-permute-start(bf16[32,16,256]{2,1,0:T(8,128)(2,1)} %get-tuple-element.162), channel_id=1, source_target_pairs={{0,1},{1,0},{2,3},{3,2},{4,5},{5,4},{6,7},{7,6}} | collective-permute-start | bytes 786440 | tf_op jit(solution)/shard_map/ppermute | solution.py:202
  27.4 62.9 %collective-permute-start.6 = (bf16[96,16,256]{2,1,0:T(8,128)(2,1)}, bf16[96,16,256]{2,1,0:T(8,128)(2,1)}, u32[]{:S(2)}, u32[]{:S(2)}) collective-permute-start(bf16[96,16,256]{2,1,0:T(8,128)(2,1)} %get-tuple-element.102), channel_id=1, source_target_pairs={{0,1},{1,0},{2,3},{3,2},{4,5},{5,4},{6,7},{7,6}} | collective-permute-start | bytes 2359304 | tf_op jit(solution)/shard_map/ppermute | solution.py:202
  30.2 60.4 %collective-permute-start.7 = (bf16[96,16,256]{2,1,0:T(8,128)(2,1)}, bf16[96,16,256]{2,1,0:T(8,128)(2,1)}, u32[]{:S(2)}, u32[]{:S(2)}) collective-permute-start(bf16[96,16,256]{2,1,0:T(8,128)(2,1)} %get-tuple-element.103), channel_id=1, source_target_pairs={{0,2},{1,3},{2,0},{3,1},{4,6},{5,7},{6,4},{7,5}} | collective-permute-start | bytes 2359304 | tf_op jit(solution)/shard_map/ppermute | solution.py:202
  31.6 59.1 %collective-permute-start.8 = (bf16[96,16,256]{2,1,0:T(8,128)(2,1)}, bf16[96,16,256]{2,1,0:T(8,128)(2,1)}, u32[]{:S(2)}, u32[]{:S(2)}) collective-permute-start(bf16[96,16,256]{2,1,0:T(8,128)(2,1)} %get-tuple-element.104), channel_id=1, source_target_pairs={{0,3},{1,2},{2,1},{3,0},{4,7},{5,6},{6,5},{7,4}} | collective-permute-start | bytes 2359304 | tf_op jit(solution)/shard_map/ppermute | solution.py:202
  31.6 47.3 %collective-permute-start.40 = (bf16[64,16,256]{2,1,0:T(8,128)(2,1)}, bf16[64,16,256]{2,1,0:T(8,128)(2,1)}, u32[]{:S(2)}, u32[]{:S(2)}) collective-permute-start(bf16[64,16,256]{2,1,0:T(8,128)(2,1)} %get-tuple-element.167), channel_id=1, source_target_pairs={{0,2},{1,3},{2,0},{3,1},{4,6},{5,7},{6,4},{7,5}} | collective-permute-start | bytes 1572872 | tf_op jit(solution)/shard_map/ppermute | solution.py:202
  33.3 55.2 %collective-permute-start.41 = (bf16[64,16,256]{2,1,0:T(8,128)(2,1)}, bf16[64,16,256]{2,1,0:T(8,128)(2,1)}, u32[]{:S(2)}, u32[]{:S(2)}) collective-permute-start(bf16[64,16,256]{2,1,0:T(8,128)(2,1)} %get-tuple-element.168), channel_id=1, source_target_pairs={{0,3},{1,2},{2,1},{3,0},{4,7},{5,6},{6,5},{7,4}} | collective-permute-start | bytes 1572872 | tf_op jit(solution)/shard_map/ppermute | solution.py:202
  79.0 27.8 %collective-permute-start.3 = (bf16[128,16,256]{2,1,0:T(8,128)(2,1)}, bf16[128,16,256]{2,1,0:T(8,128)(2,1)}, u32[]{:S(2)}, u32[]{:S(2)}) collective-permute-start(bf16[128,16,256]{2,1,0:T(8,128)(2,1)} %get-tuple-element.98), channel_id=1, source_target_pairs={{0,1},{1,0},{2,3},{3,2},{4,5},{5,4},{6,7},{7,6}} | collective-permute-start | bytes 3145736 | tf_op jit(solution)/shard_map/ppermute | solution.py:202
  88.5 26.3 %collective-permute-start.4 = (bf16[128,16,256]{2,1,0:T(8,128)(2,1)}, bf16[128,16,256]{2,1,0:T(8,128)(2,1)}, u32[]{:S(2)}, u32[]{:S(2)}) collective-permute-start(bf16[128,16,256]{2,1,0:T(8,128)(2,1)} %get-tuple-element.99), channel_id=1, source_target_pairs={{0,2},{1,3},{2,0},{3,1},{4,6},{5,7},{6,4},{7,5}} | collective-permute-start | bytes 3145736 | tf_op jit(solution)/shard_map/ppermute | solution.py:202
  90.3 46.4 %collective-permute-start.5 = (bf16[128,16,256]{2,1,0:T(8,128)(2,1)}, bf16[128,16,256]{2,1,0:T(8,128)(2,1)}, u32[]{:S(2)}, u32[]{:S(2)}) collective-permute-start(bf16[128,16,256]{2,1,0:T(8,128)(2,1)} %get-tuple-element.100), channel_id=1, source_target_pairs={{0,3},{1,2},{2,1},{3,0},{4,7},{5,6},{6,5},{7,4}} | collective-permute-start | bytes 3145736 | tf_op jit(solution)/shard_map/ppermute | solution.py:202
  90.5 47.7 %collective-permute-start.12 = (bf16[128,16,256]{2,1,0:T(8,128)(2,1)}, bf16[128,16,256]{2,1,0:T(8,128)(2,1)}, u32[]{:S(2)}, u32[]{:S(2)}) collective-permute-start(bf16[128,16,256]{2,1,0:T(8,128)(2,1)} %get-tuple-element.116), channel_id=1, source_target_pairs={{0,1},{1,0},{2,3},{3,2},{4,5},{5,4},{6,7},{7,6}} | collective-permute-start | bytes 3145736 | tf_op jit(solution)/shard_map/ppermute | solution.py:202
  90.7 69.1 %collective-permute-start.13 = (bf16[128,16,256]{2,1,0:T(8,128)(2,1)}, bf16[128,16,256]{2,1,0:T(8,128)(2,1)}, u32[]{:S(2)}, u32[]{:S(2)}) collective-permute-start(bf16[128,16,256]{2,1,0:T(8,128)(2,1)} %get-tuple-element.117), channel_id=1, source_target_pairs={{0,2},{1,3},{2,0},{3,1},{4,6},{5,7},{6,4},{7,5}} | collective-permute-start | bytes 3145736 | tf_op jit(solution)/shard_map/ppermute | solution.py:202
  106.8 74.9 %collective-permute-start.14 = (bf16[128,16,256]{2,1,0:T(8,128)(2,1)}, bf16[128,16,256]{2,1,0:T(8,128)(2,1)}, u32[]{:S(2)}, u32[]{:S(2)}) collective-permute-start(bf16[128,16,256]{2,1,0:T(8,128)(2,1)} %get-tuple-element.118), channel_id=1, source_target_pairs={{0,3},{1,2},{2,1},{3,0},{4,7},{5,6},{6,5},{7,4}} | collective-permute-start | bytes 3145736 | tf_op jit(solution)/shard_map/ppermute | solution.py:202
  114.9 68.3 %collective-permute-start = (bf16[128,16,256]{2,1,0:T(8,128)(2,1)}, bf16[128,16,256]{2,1,0:T(8,128)(2,1)}, u32[]{:S(2)}, u32[]{:S(2)}) collective-permute-start(bf16[128,16,256]{2,1,0:T(8,128)(2,1)} %get-tuple-element.94), channel_id=1, source_target_pairs={{0,1},{1,0},{2,3},{3,2},{4,5},{5,4},{6,7},{7,6}} | collective-permute-start | bytes 3145736 | tf_op jit(solution)/shard_map/ppermute | solution.py:202
  136.7 68.0 %collective-permute-start.1 = (bf16[128,16,256]{2,1,0:T(8,128)(2,1)}, bf16[128,16,256]{2,1,0:T(8,128)(2,1)}, u32[]{:S(2)}, u32[]{:S(2)}) collective-permute-start(bf16[128,16,256]{2,1,0:T(8,128)(2,1)} %get-tuple-element.95), channel_id=1, source_target_pairs={{0,2},{1,3},{2,0},{3,1},{4,6},{5,7},{6,4},{7,5}} | collective-permute-start | bytes 3145736 | tf_op jit(solution)/shard_map/ppermute | solution.py:202
  138.2 88.4 %collective-permute-start.2 = (bf16[128,16,256]{2,1,0:T(8,128)(2,1)}, bf16[128,16,256]{2,1,0:T(8,128)(2,1)}, u32[]{:S(2)}, u32[]{:S(2)}) collective-permute-start(bf16[128,16,256]{2,1,0:T(8,128)(2,1)} %get-tuple-element.96), channel_id=1, source_target_pairs={{0,3},{1,2},{2,1},{3,0},{4,7},{5,6},{6,5},{7,4}} | collective-permute-start | bytes 3145736 | tf_op jit(solution)/shard_map/ppermute | solution.py:202
  159.8 68.3 %collective-permute-start.21 = (bf16[128,16,256]{2,1,0:T(8,128)(2,1)}, bf16[128,16,256]{2,1,0:T(8,128)(2,1)}, u32[]{:S(2)}, u32[]{:S(2)}) collective-permute-start(bf16[128,16,256]{2,1,0:T(8,128)(2,1)} %get-tuple-element.131), channel_id=1, source_target_pairs={{0,1},{1,0},{2,3},{3,2},{4,5},{5,4},{6,7},{7,6}} | collective-permute-start | bytes 3145736 | tf_op jit(solution)/shard_map/ppermute | solution.py:202
  181.7 68.0 %collective-permute-start.22 = (bf16[128,16,256]{2,1,0:T(8,128)(2,1)}, bf16[128,16,256]{2,1,0:T(8,128)(2,1)}, u32[]{:S(2)}, u32[]{:S(2)}) collective-permute-start(bf16[128,16,256]{2,1,0:T(8,128)(2,1)} %get-tuple-element.132), channel_id=1, source_target_pairs={{0,2},{1,3},{2,0},{3,1},{4,6},{5,7},{6,4},{7,5}} | collective-permute-start | bytes 3145736 | tf_op jit(solution)/shard_map/ppermute | solution.py:202
  183.2 88.4 %collective-permute-start.23 = (bf16[128,16,256]{2,1,0:T(8,128)(2,1)}, bf16[128,16,256]{2,1,0:T(8,128)(2,1)}, u32[]{:S(2)}, u32[]{:S(2)}) collective-permute-start(bf16[128,16,256]{2,1,0:T(8,128)(2,1)} %get-tuple-element.133), channel_id=1, source_target_pairs={{0,3},{1,2},{2,1},{3,0},{4,7},{5,6},{6,5},{7,4}} | collective-permute-start | bytes 3145736 | tf_op jit(solution)/shard_map/ppermute | solution.py:202
  204.8 68.3 %collective-permute-start.18 = (bf16[128,16,256]{2,1,0:T(8,128)(2,1)}, bf16[128,16,256]{2,1,0:T(8,128)(2,1)}, u32[]{:S(2)}, u32[]{:S(2)}) collective-permute-start(bf16[128,16,256]{2,1,0:T(8,128)(2,1)} %get-tuple-element.127), channel_id=1, source_target_pairs={{0,1},{1,0},{2,3},{3,2},{4,5},{5,4},{6,7},{7,6}} | collective-permute-start | bytes 3145736 | tf_op jit(solution)/shard_map/ppermute | solution.py:202
  226.6 68.0 %collective-permute-start.19 = (bf16[128,16,256]{2,1,0:T(8,128)(2,1)}, bf16[128,16,256]{2,1,0:T(8,128)(2,1)}, u32[]{:S(2)}, u32[]{:S(2)}) collective-permute-start(bf16[128,16,256]{2,1,0:T(8,128)(2,1)} %get-tuple-element.128), channel_id=1, source_target_pairs={{0,2},{1,3},{2,0},{3,1},{4,6},{5,7},{6,4},{7,5}} | collective-permute-start | bytes 3145736 | tf_op jit(solution)/shard_map/ppermute | solution.py:202
  228.1 88.4 %collective-permute-start.20 = (bf16[128,16,256]{2,1,0:T(8,128)(2,1)}, bf16[128,16,256]{2,1,0:T(8,128)(2,1)}, u32[]{:S(2)}, u32[]{:S(2)}) collective-permute-start(bf16[128,16,256]{2,1,0:T(8,128)(2,1)} %get-tuple-element.129), channel_id=1, source_target_pairs={{0,3},{1,2},{2,1},{3,0},{4,7},{5,6},{6,5},{7,4}} | collective-permute-start | bytes 3145736 | tf_op jit(solution)/shard_map/ppermute | solution.py:202
  249.7 90.4 %collective-permute-start.24 = (bf16[128,16,256]{2,1,0:T(8,128)(2,1)}, bf16[128,16,256]{2,1,0:T(8,128)(2,1)}, u32[]{:S(2)}, u32[]{:S(2)}) collective-permute-start(bf16[128,16,256]{2,1,0:T(8,128)(2,1)} %get-tuple-element.139), channel_id=1, source_target_pairs={{0,1},{1,0},{2,3},{3,2},{4,5},{5,4},{6,7},{7,6}} | collective-permute-start | bytes 3145736 | tf_op jit(solution)/shard_map/ppermute | solution.py:202
  271.5 68.9 %collective-permute-start.25 = (bf16[128,16,256]{2,1,0:T(8,128)(2,1)}, bf16[128,16,256]{2,1,0:T(8,128)(2,1)}, u32[]{:S(2)}, u32[]{:S(2)}) collective-permute-start(bf16[128,16,256]{2,1,0:T(8,128)(2,1)} %get-tuple-element.140), channel_id=1, source_target_pairs={{0,2},{1,3},{2,0},{3,1},{4,6},{5,7},{6,4},{7,5}} | collective-permute-start | bytes 3145736 | tf_op jit(solution)/shard_map/ppermute | solution.py:202
  273.0 88.4 %collective-permute-start.26 = (bf16[128,16,256]{2,1,0:T(8,128)(2,1)}, bf16[128,16,256]{2,1,0:T(8,128)(2,1)}, u32[]{:S(2)}, u32[]{:S(2)}) collective-permute-start(bf16[128,16,256]{2,1,0:T(8,128)(2,1)} %get-tuple-element.141), channel_id=1, source_target_pairs={{0,3},{1,2},{2,1},{3,0},{4,7},{5,6},{6,5},{7,4}} | collective-permute-start | bytes 3145736 | tf_op jit(solution)/shard_map/ppermute | solution.py:202
  294.6 68.3 %collective-permute-start.15 = (bf16[128,16,256]{2,1,0:T(8,128)(2,1)}, bf16[128,16,256]{2,1,0:T(8,128)(2,1)}, u32[]{:S(2)}, u32[]{:S(2)}) collective-permute-start(bf16[128,16,256]{2,1,0:T(8,128)(2,1)} %get-tuple-element.123), channel_id=1, source_target_pairs={{0,1},{1,0},{2,3},{3,2},{4,5},{5,4},{6,7},{7,6}} | collective-permute-start | bytes 3145736 | tf_op jit(solution)/shard_map/ppermute | solution.py:202
  316.5 68.0 %collective-permute-start.16 = (bf16[128,16,256]{2,1,0:T(8,128)(2,1)}, bf16[128,16,256]{2,1,0:T(8,128)(2,1)}, u32[]{:S(2)}, u32[]{:S(2)}) collective-permute-start(bf16[128,16,256]{2,1,0:T(8,128)(2,1)} %get-tuple-element.124), channel_id=1, source_target_pairs={{0,2},{1,3},{2,0},{3,1},{4,6},{5,7},{6,4},{7,5}} | collective-permute-start | bytes 3145736 | tf_op jit(solution)/shard_map/ppermute | solution.py:202
  334.5 0.6 copy-start
  340.1 66.2 %collective-permute-start.17 = (bf16[128,16,256]{2,1,0:T(8,128)(2,1)}, bf16[128,16,256]{2,1,0:T(8,128)(2,1)}, u32[]{:S(2)}, u32[]{:S(2)}) collective-permute-start(bf16[128,16,256]{2,1,0:T(8,128)(2,1)} %get-tuple-element.125), channel_id=1, source_target_pairs={{0,3},{1,2},{2,1},{3,0},{4,7},{5,6},{6,5},{7,4}} | collective-permute-start | bytes 3145736 | tf_op jit(solution)/shard_map/ppermute | solution.py:202
  340.4 67.4 %collective-permute-start.33 = (bf16[128,16,256]{2,1,0:T(8,128)(2,1)}, bf16[128,16,256]{2,1,0:T(8,128)(2,1)}, u32[]{:S(2)}, u32[]{:S(2)}) collective-permute-start(bf16[128,16,256]{2,1,0:T(8,128)(2,1)} %get-tuple-element.154), channel_id=1, source_target_pairs={{0,1},{1,0},{2,3},{3,2},{4,5},{5,4},{6,7},{7,6}} | collective-permute-start | bytes 3145736 | tf_op jit(solution)/shard_map/ppermute | solution.py:202
  361.4 68.0 %collective-permute-start.34 = (bf16[128,16,256]{2,1,0:T(8,128)(2,1)}, bf16[128,16,256]{2,1,0:T(8,128)(2,1)}, u32[]{:S(2)}, u32[]{:S(2)}) collective-permute-start(bf16[128,16,256]{2,1,0:T(8,128)(2,1)} %get-tuple-element.155), channel_id=1, source_target_pairs={{0,2},{1,3},{2,0},{3,1},{4,6},{5,7},{6,4},{7,5}} | collective-permute-start | bytes 3145736 | tf_op jit(solution)/shard_map/ppermute | solution.py:202
  362.9 88.4 %collective-permute-start.35 = (bf16[128,16,256]{2,1,0:T(8,128)(2,1)}, bf16[128,16,256]{2,1,0:T(8,128)(2,1)}, u32[]{:S(2)}, u32[]{:S(2)}) collective-permute-start(bf16[128,16,256]{2,1,0:T(8,128)(2,1)} %get-tuple-element.156), channel_id=1, source_target_pairs={{0,3},{1,2},{2,1},{3,0},{4,7},{5,6},{6,5},{7,4}} | collective-permute-start | bytes 3145736 | tf_op jit(solution)/shard_map/ppermute | solution.py:202
  384.5 68.3 %collective-permute-start.30 = (bf16[128,16,256]{2,1,0:T(8,128)(2,1)}, bf16[128,16,256]{2,1,0:T(8,128)(2,1)}, u32[]{:S(2)}, u32[]{:S(2)}) collective-permute-start(bf16[128,16,256]{2,1,0:T(8,128)(2,1)} %get-tuple-element.150), channel_id=1, source_target_pairs={{0,1},{1,0},{2,3},{3,2},{4,5},{5,4},{6,7},{7,6}} | collective-permute-start | bytes 3145736 | tf_op jit(solution)/shard_map/ppermute | solution.py:202
  406.4 87.8 %collective-permute-start.31 = (bf16[128,16,256]{2,1,0:T(8,128)(2,1)}, bf16[128,16,256]{2,1,0:T(8,128)(2,1)}, u32[]{:S(2)}, u32[]{:S(2)}) collective-permute-start(bf16[128,16,256]{2,1,0:T(8,128)(2,1)} %get-tuple-element.151), channel_id=1, source_target_pairs={{0,2},{1,3},{2,0},{3,1},{4,6},{5,7},{6,4},{7,5}} | collective-permute-start | bytes 3145736 | tf_op jit(solution)/shard_map/ppermute | solution.py:202
  407.9 88.4 %collective-permute-start.32 = (bf16[128,16,256]{2,1,0:T(8,128)(2,1)}, bf16[128,16,256]{2,1,0:T(8,128)(2,1)}, u32[]{:S(2)}, u32[]{:S(2)}) collective-permute-start(bf16[128,16,256]{2,1,0:T(8,128)(2,1)} %get-tuple-element.152), channel_id=1, source_target_pairs={{0,3},{1,2},{2,1},{3,0},{4,7},{5,6},{6,5},{7,4}} | collective-permute-start | bytes 3145736 | tf_op jit(solution)/shard_map/ppermute | solution.py:202
  429.5 68.6 %collective-permute-start.42 = (bf16[128,16,256]{2,1,0:T(8,128)(2,1)}, bf16[128,16,256]{2,1,0:T(8,128)(2,1)}, u32[]{:S(2)}, u32[]{:S(2)}) collective-permute-start(bf16[128,16,256]{2,1,0:T(8,128)(2,1)} %get-tuple-element.170), channel_id=1, source_target_pairs={{0,1},{1,0},{2,3},{3,2},{4,5},{5,4},{6,7},{7,6}} | collective-permute-start | bytes 3145736 | tf_op jit(solution)/shard_map/ppermute | solution.py:202
  451.3 68.0 %collective-permute-start.43 = (bf16[128,16,256]{2,1,0:T(8,128)(2,1)}, bf16[128,16,256]{2,1,0:T(8,128)(2,1)}, u32[]{:S(2)}, u32[]{:S(2)}) collective-permute-start(bf16[128,16,256]{2,1,0:T(8,128)(2,1)} %get-tuple-element.171), channel_id=1, source_target_pairs={{0,2},{1,3},{2,0},{3,1},{4,6},{5,7},{6,4},{7,5}} | collective-permute-start | bytes 3145736 | tf_op jit(solution)/shard_map/ppermute | solution.py:202
  452.8 88.4 %collective-permute-start.44 = (bf16[128,16,256]{2,1,0:T(8,128)(2,1)}, bf16[128,16,256]{2,1,0:T(8,128)(2,1)}, u32[]{:S(2)}, u32[]{:S(2)}) collective-permute-start(bf16[128,16,256]{2,1,0:T(8,128)(2,1)} %get-tuple-element.172), channel_id=1, source_target_pairs={{0,3},{1,2},{2,1},{3,0},{4,7},{5,6},{6,5},{7,4}} | collective-permute-start | bytes 3145736 | tf_op jit(solution)/shard_map/ppermute | solution.py:202
  494.2 106.4 %collective-permute-start.37 = (bf16[32,16,256]{2,1,0:T(8,128)(2,1)}, bf16[32,16,256]{2,1,0:T(8,128)(2,1)}, u32[]{:S(2)}, u32[]{:S(2)}) collective-permute-start(bf16[32,16,256]{2,1,0:T(8,128)(2,1)} %get-tuple-element.163), channel_id=1, source_target_pairs={{0,2},{1,3},{2,0},{3,1},{4,6},{5,7},{6,4},{7,5}} | collective-permute-start | bytes 786440 | tf_op jit(solution)/shard_map/ppermute | solution.py:202
  496.3 104.3 %collective-permute-start.38 = (bf16[32,16,256]{2,1,0:T(8,128)(2,1)}, bf16[32,16,256]{2,1,0:T(8,128)(2,1)}, u32[]{:S(2)}, u32[]{:S(2)}) collective-permute-start(bf16[32,16,256]{2,1,0:T(8,128)(2,1)} %get-tuple-element.164), channel_id=1, source_target_pairs={{0,3},{1,2},{2,1},{3,0},{4,7},{5,6},{6,5},{7,4}} | collective-permute-start | bytes 786440 | tf_op jit(solution)/shard_map/ppermute | solution.py:202
  498.1 105.9 %collective-permute-start.27 = (bf16[32,16,256]{2,1,0:T(8,128)(2,1)}, bf16[32,16,256]{2,1,0:T(8,128)(2,1)}, u32[]{:S(2)}, u32[]{:S(2)}) collective-permute-start(bf16[32,16,256]{2,1,0:T(8,128)(2,1)} %get-tuple-element.146), channel_id=1, source_target_pairs={{0,1},{1,0},{2,3},{3,2},{4,5},{5,4},{6,7},{7,6}} | collective-permute-start | bytes 786440 | tf_op jit(solution)/shard_map/ppermute | solution.py:202
  519.4 84.7 %collective-permute-start.28 = (bf16[32,16,256]{2,1,0:T(8,128)(2,1)}, bf16[32,16,256]{2,1,0:T(8,128)(2,1)}, u32[]{:S(2)}, u32[]{:S(2)}) collective-permute-start(bf16[32,16,256]{2,1,0:T(8,128)(2,1)} %get-tuple-element.147), channel_id=1, source_target_pairs={{0,2},{1,3},{2,0},{3,1},{4,6},{5,7},{6,4},{7,5}} | collective-permute-start | bytes 786440 | tf_op jit(solution)/shard_map/ppermute | solution.py:202
  541.2 62.8 %collective-permute-start.29 = (bf16[32,16,256]{2,1,0:T(8,128)(2,1)}, bf16[32,16,256]{2,1,0:T(8,128)(2,1)}, u32[]{:S(2)}, u32[]{:S(2)}) collective-permute-start(bf16[32,16,256]{2,1,0:T(8,128)(2,1)} %get-tuple-element.148), channel_id=1, source_target_pairs={{0,3},{1,2},{2,1},{3,0},{4,7},{5,6},{6,5},{7,4}} | collective-permute-start | bytes 786440 | tf_op jit(solution)/shard_map/ppermute | solution.py:202
